TPU v7x, 128 devices: a whole 4x4x4 slice. The times are simulated.
128 devices in a mesh: seq: 32 (over z, y_hi, x), head: 4 (over y_lo, core).
Axes of the slice: x: 4, y: 4 (y_hi: 2, y_lo: 2; y = y_hi * 2 + y_lo), z: 4, core: 2. Of those that a mesh axis runs over, the one named last changes fastest.
Arguments:
- queries: bfloat16 [8192, 3584], P('seq', 'head'), may hold values from -5 to 5
- keys: bfloat16 [8192, 3584], P('seq', 'head'), may hold values from -5 to 5
- values: bfloat16 [8192, 3584], P('seq', 'head'), may hold values from -6 to 6
- attn_grad: bfloat16 [8192, 3584], P('seq', 'head'), may hold values from -6 to 6
- doc_ids: int32 [8192], replicated, may hold values from 0 to 7, never falling along the last dimension, each value on 1 to 4096 neighbouring positions
- conv_input: bfloat16 [8192, 7168], P('seq', 'head'), may hold values from -6 to 6
- conv_weight: float32 [4, 7168], P(None, 'head'), may hold values from -3 to 3
- step_raw: float32 [8192, 112], P('seq', 'head'), may hold values from -4 to 4
- step_bias: float32 [112], P('head'), may hold values from -1.5 to 0
- rate_log: float32 [112], P('head'), may hold values from -13 to -1
- skip_gain: float32 [112], P('head'), may hold values from 0.5 to 1.5
- input_coeff: bfloat16 [8192, 128], P('seq'), may hold values from -0.625 to 0.625
- output_coeff: bfloat16 [8192, 128], P('seq'), may hold values from -0.625 to 0.625
- gate_input: bfloat16 [8192, 7168], P('seq', 'head'), may hold values from -6 to 6
- mix_grad: bfloat16 [8192, 7168], P('seq', 'head'), may hold values from -1.5 to 1.5
Outputs:
- grad_queries: bfloat16 [8192, 3584], P('seq', 'head')
- grad_keys: bfloat16 [8192, 3584], P('seq', 'head')
- grad_values: bfloat16 [8192, 3584], P('seq', 'head')
- grad_conv_input: bfloat16 [8192, 7168], P('seq', 'head')
- grad_gate: bfloat16 [8192, 7168], P('seq', 'head')
- grad_step: float32 [8192, 112], P('seq', 'head')
- grad_input_coeff: float32 [8192, 128], P('seq')
- grad_output_coeff: float32 [8192, 128], P('seq')
- grad_conv_weight: float32 [4, 7168], P(None, 'head')
- grad_step_bias: float32 [112], P('head')
- grad_rate_log: float32 [112], P('head')
- grad_skip: float32 [112], P('head')
Inputs may be any that keep to these rules, and one draw needn't show every extreme that they name: doc_ids never fall along the sequence.
All inputs are finite; a program needn't handle non-finite values.
Results may differ from a plain program's by a relative error of at most 0.012.
Values may be sent and summed in bfloat16 or wider, within the bound.
A program may use at most 128 MiB of HBM per device.

v0:
```python
import jax
import jax.numpy as jnp
from jax import lax
from jax.experimental import pallas as pl
from jax.experimental.pallas import tpu as pltpu
from jax.sharding import PartitionSpec as P

HEAD_DIM = 224
WINDOW = 1024
KERNEL = 4
PAD = 8
LANES = 128
PLACES = 4
DOCS = 8
REACH = 4

EXACT = lax.Precision.HIGHEST
F32 = jnp.float32
BF16 = jnp.bfloat16
NEG_FILL = -1e30
SCALE = HEAD_DIM ** (-0.5)


def dot(a, b, ca, cb, precision=None):
    return lax.dot_general(
        a, b, (((ca,), (cb,)), ((), ())), preferred_element_type=F32, precision=precision
    )


def where_am_i():
    index = lax.axis_index("seq")
    groups = lax.axis_size("seq") // PLACES
    return lax.div(index, PLACES), lax.rem(index, PLACES), groups


def shard(group, place, groups):
    return {"seq": lax.rem(group + 2 * groups, groups) * PLACES + place}


def greet(partners):
    barrier = pltpu.get_barrier_semaphore()
    for partner in partners:
        pl.semaphore_signal(barrier, inc=1, device_id=partner, device_id_type=pl.DeviceIdType.MESH)
    return lambda: pl.semaphore_wait(barrier, len(partners))


class Post:
    def __init__(self, sends, receives):
        self.sends, self.receives, self.used = sends, receives, 0

    def send(self, source, target, device):
        copy = pltpu.make_async_remote_copy(
            src_ref=source, dst_ref=target, send_sem=self.sends.at[self.used],
            recv_sem=self.receives.at[self.used], device_id=device,
            device_id_type=pl.DeviceIdType.MESH,
        )
        self.used += 1
        copy.start()
        return copy


def spreader(heads, channels):
    width = channels // heads
    row = lax.broadcasted_iota(jnp.int32, (LANES, channels), 0)
    col = lax.broadcasted_iota(jnp.int32, (LANES, channels), 1)
    return ((col >= row * width) & (col < row * width + width)).astype(F32)


def causal(rows):
    i = lax.broadcasted_iota(jnp.int32, (rows, rows), 0)
    j = lax.broadcasted_iota(jnp.int32, (rows, rows), 1)
    return i, j


def pair_columns(cols, index, lower):
    return jnp.where(lower, cols[:, 2 * index : 2 * index + 1], cols[:, 2 * index + 1 : 2 * index + 2])


def fill_masks(since_ref, mask_ref):
    for lag in range(1, KERNEL):
        mask_ref[lag - 1] = jnp.broadcast_to((since_ref[...] >= lag).astype(F32), mask_ref.shape[1:])


def conv_pre(conv, tail, wt, mask_ref, xp_ref):
    rows = conv.shape[0]
    xp_ref[:PAD, :] = tail.astype(F32)[PAD:]
    xp_ref[PAD:, :] = conv.astype(F32)
    pre = wt[0:1, :] * xp_ref[PAD:, :]
    for lag in range(1, KERNEL):
        pre = pre + wt[lag : lag + 1, :] * (xp_ref[PAD - lag : PAD - lag + rows, :] * mask_ref[lag - 1])
    return pre


def group_part(ref):
    half = ref.shape[1] // 2
    whole = ref[...].astype(F32)
    first = lax.axis_index("head") < lax.axis_size("head") // 2
    return jnp.where(first, whole[:, :half], whole[:, half:]).astype(BF16)


def pre_kernel(
    q_ref, k_ref, v_ref, do_ref, since_ref, step_ref, bias_ref, rate_ref, b_ref, c_ref, wt_ref,
    conv_hbm, gate_hbm, mix_hbm,
    recv_ref, prev_ref, cols_ref, rowc_ref, through_ref, state_ref, tail_ref,
    pack_ref, conv_ref, gate_ref, mix_ref, tail_buf, spread_ref, mask_ref, xp_ref,
    ends_ref, a_ref, end_out, cot_out, g_out, e_in, c_in, ge_in, gc_in, back_ref, state_buf, t_out, t_all,
    sends, receives, loads, locals_,
):
    group, place, groups = where_am_i()
    rows, heads = step_ref.shape
    channels = conv_ref.shape[1]
    pairs = channels // LANES
    peers = [lax.rem(place + d, PLACES) for d in range(1, PLACES)]
    post = Post(sends, receives)
    partners = [shard(group, peer, groups) for peer in peers]
    partners += [shard(group + side, other, groups) for side in (1, -1) for other in range(PLACES)]
    partners += [shard(group + far, place, groups) for far in range(2, groups - 1)]
    wait_partners = greet(partners)

    fetches = [
        pltpu.make_async_copy(source, target, loads.at[n])
        for n, (source, target) in enumerate(
            ((conv_hbm, conv_ref), (gate_hbm, gate_ref), (mix_hbm, mix_ref))
        )
    ]
    for fetch in fetches:
        fetch.start()
    for n, ref in enumerate((q_ref, do_ref, k_ref, v_ref)):
        for r in range(PLACES):
            pack_ref[r, :, n * HEAD_DIM : (n + 1) * HEAD_DIM] = ref[:, r * HEAD_DIM : (r + 1) * HEAD_DIM]
    fetches[0].wait()
    wait_partners()

    last = place == PLACES - 1
    follower = shard(jnp.where(last, group + 1, group), lax.rem(place + 1, PLACES), groups)
    tail_copy = post.send(conv_ref.at[rows - 2 * PAD :, :], tail_buf, follower)
    bulk = []
    for r in [place] + peers:
        bulk.append(post.send(pack_ref.at[r, :, 3 * LANES :], prev_ref.at[place], shard(group + 1, r, groups)))
    for peer in peers:
        bulk.append(post.send(pack_ref.at[peer], recv_ref.at[place], shard(group, peer, groups)))
    keep = pltpu.make_async_copy(pack_ref.at[place], recv_ref.at[place], locals_.at[0])
    keep.start()

    since = since_ref[...]
    raw = step_ref[...] + bias_ref[...]
    step = jnp.maximum(raw, 0.0) + jnp.log1p(jnp.exp(-jnp.abs(raw)))
    log_decay = -step * jnp.exp(rate_ref[...])
    i, j = causal(rows)
    tri = (i >= j).astype(F32)
    cum = dot(tri, log_decay, 1, 0, EXACT)
    row_cum = dot(log_decay, tri, 0, 1, EXACT)
    t = lax.broadcasted_iota(jnp.int32, (rows, 1), 0).astype(F32)
    enter = jnp.where(since > t, jnp.exp(cum), 0.0)
    final = cum[rows - 1 : rows]
    to_end = jnp.where((rows - 1) - t <= since[rows - 1 : rows], jnp.exp(final - cum), 0.0)
    through = enter[rows - 1 : rows]
    t_out[...] = jnp.zeros_like(t_out)
    t_out[0:1, 0:heads] = through
    through_ref[...] = through
    t_all[place] = t_out[...]
    t_copies = [post.send(t_out, t_all.at[place], shard(group, peer, groups)) for peer in peers]
    for n in range(pairs):
        two = slice(2 * n, 2 * n + 2)
        cols_ref[n] = jnp.concatenate([cum[:, two], step[:, two], enter[:, two], to_end[:, two]], axis=1)
        rowc_ref[n] = row_cum[two]
    spread_ref[...] = spreader(heads, channels)
    fill_masks(since_ref, mask_ref)
    lower = lax.broadcasted_iota(jnp.int32, (rows, LANES), 1) < LANES // 2
    b_part, c_part = group_part(b_ref), group_part(c_ref)
    fetches[1].wait()
    fetches[2].wait()
    tail_copy.wait()
    tail_ref[...] = tail_buf[...]

    def ends(n, carry):
        lanes = pl.ds(pl.multiple_of(n * LANES, LANES), LANES)
        cols = cols_ref[n]
        pre = conv_pre(conv_ref[:, lanes], tail_buf[:, lanes], wt_ref[:, lanes], mask_ref, xp_ref)
        act = pre * jax.nn.sigmoid(pre)
        weighted = act * pair_columns(cols, 1, lower) * pair_columns(cols, 3, lower)
        end = dot(b_part, weighted.astype(BF16), 0, 0).astype(BF16)
        gate = gate_ref[:, lanes].astype(F32)
        dy = mix_ref[:, lanes].astype(F32) * (gate * jax.nn.sigmoid(gate))
        start = dot(c_part, (dy * pair_columns(cols, 2, lower)).astype(BF16), 0, 0).astype(BF16)
        for r in range(PLACES):
            part = slice(2 * PAD * r, 2 * PAD * (r + 1))
            ends_ref[r, 0, :, lanes] = end[part]
            ends_ref[r, 1, :, lanes] = start[part]
        return carry

    lax.fori_loop(0, pairs, ends, 0)

    a_copies = [post.send(ends_ref.at[peer], a_ref.at[place], shard(group, peer, groups)) for peer in peers]
    a_ref[place] = ends_ref[place]
    for copy in t_copies + a_copies:
        copy.wait()
    decays = dot(t_all[...].reshape(PLACES * PAD, LANES), spread_ref[...], 1, 0, EXACT)
    decay = [decays[PAD * n : PAD * n + 1] for n in range(PLACES)]
    end_of = lambda n: a_ref[n, 0].astype(F32)
    cot_of = lambda n: a_ref[n, 1].astype(F32)
    end, cot = end_of(0), cot_of(PLACES - 1)
    for n in range(1, PLACES):
        end = end_of(n) + decay[n] * end
        cot = cot_of(PLACES - 1 - n) + decay[PLACES - 1 - n] * cot
    end_out[...] = end.astype(BF16)
    cot_out[...] = cot.astype(BF16)
    g_out[...] = t_all[0] * t_all[1] * t_all[2] * t_all[3]
    b_copies = []
    for far in range(1, REACH + 1):
        later, earlier = shard(group + far, place, groups), shard(group - far, place, groups)
        b_copies.append(post.send(end_out, e_in.at[far - 1], later))
        b_copies.append(post.send(g_out, ge_in.at[far - 1], later))
        b_copies.append(post.send(cot_out, c_in.at[far - 1], earlier))
        b_copies.append(post.send(g_out, gc_in.at[far - 1], earlier))
    for copy in b_copies:
        copy.wait()
    before = dot(ge_in[...].reshape(REACH * PAD, LANES), spread_ref[...], 1, 0, EXACT)
    after = dot(gc_in[...].reshape(REACH * PAD, LANES), spread_ref[...], 1, 0, EXACT)
    state = e_in[REACH - 1].astype(F32)
    cot = c_in[REACH - 1].astype(F32) * (group + REACH < groups).astype(F32)
    for far in range(REACH - 2, -1, -1):
        state = e_in[far].astype(F32) + before[PAD * far : PAD * far + 1] * state
        cot = (c_in[far].astype(F32) + after[PAD * far : PAD * far + 1] * cot) * (
            group + far + 1 < groups
        ).astype(F32)
    for n in range(PLACES):
        back_ref[n, 0] = state.astype(BF16)
        state = end_of(n) + decay[n] * state
        m = PLACES - 1 - n
        back_ref[m, 1] = cot.astype(BF16)
        cot = cot_of(m) + decay[m] * cot
    final_copies = [
        post.send(back_ref.at[peer], state_buf.at[place], shard(group, peer, groups)) for peer in peers
    ]
    state_buf[place] = back_ref[place]
    for copy in final_copies:
        copy.wait()
    state_ref[...] = state_buf[...]
    for copy in bulk:
        copy.wait()
    keep.wait()


def attn_kernel(low_ref, recv_ref, prev_ref, own_ref, back_ref, q_all, do_all, k_all, v_all, dk_all, dv_all):
    places, rows, _ = recv_ref.shape
    span = places * rows
    for r in range(places):
        here, later = slice(r * rows, (r + 1) * rows), slice(span + r * rows, span + (r + 1) * rows)
        q_all[here, :] = recv_ref[r, :, 0:HEAD_DIM]
        do_all[here, :] = recv_ref[r, :, HEAD_DIM : 2 * HEAD_DIM]
        k_all[later, :] = recv_ref[r, :, 2 * HEAD_DIM : 3 * HEAD_DIM]
        v_all[later, :] = recv_ref[r, :, 3 * HEAD_DIM : 4 * HEAD_DIM]
        skip = 2 * HEAD_DIM - 3 * LANES
        k_all[here, :] = prev_ref[r, :, skip : skip + HEAD_DIM]
        v_all[here, :] = prev_ref[r, :, skip + HEAD_DIM : skip + 2 * HEAD_DIM]
    dk_all[...] = jnp.zeros_like(dk_all)
    dv_all[...] = jnp.zeros_like(dv_all)
    j = lax.broadcasted_iota(jnp.int32, (rows, rows), 0)
    i = lax.broadcasted_iota(jnp.int32, (rows, rows), 1)

    def block(b, carry):
        mine = pl.ds(pl.multiple_of(b * rows, rows), rows)
        q = q_all[mine, :]
        grad = do_all[mine, :]
        low = low_ref[pl.ds(b, 1), :]
        at = [pl.ds(pl.multiple_of((b + places - gap) * rows, rows), rows) for gap in range(places + 1)]
        scores = []
        top = None
        for gap in range(places + 1):
            allowed = j + (b + places - gap) * rows >= low
            if gap == 0:
                allowed = allowed & (i >= j)
            s = jnp.where(allowed, dot(k_all[at[gap], :], q, 1, 1) * SCALE, NEG_FILL)
            scores.append(s)
            m = jnp.max(s, axis=0, keepdims=True)
            top = m if top is None else jnp.maximum(top, m)
        total = None
        expo = []
        for gap in range(places + 1):
            e = jnp.exp(scores[gap] - top)
            expo.append(e)
            t = jnp.sum(e, axis=0, keepdims=True)
            total = t if total is None else total + t
        inverse = 1.0 / jnp.maximum(total, 1.0)
        delta = None
        dprobs = []
        for gap in range(places + 1):
            half = (expo[gap] * inverse).astype(BF16)
            dp = dot(v_all[at[gap], :], grad, 1, 1)
            d = jnp.sum(half.astype(F32) * dp, axis=0, keepdims=True)
            delta = d if delta is None else delta + d
            dv_all[at[gap], :] += dot(half, grad, 1, 0)
            dprobs.append(dp)
        dq = None
        for gap in range(places + 1):
            ds = (expo[gap] * inverse * (dprobs[gap] - delta)).astype(BF16)
            dk_all[at[gap], :] += dot(ds, q, 1, 0)
            part = dot(ds, k_all[at[gap], :], 0, 0)
            dq = part if dq is None else dq + part
        own_ref[b, :, 0:HEAD_DIM] = (dq * SCALE).astype(BF16)
        return carry

    lax.fori_loop(0, places, block, 0)
    for r in range(places):
        here, later = slice(r * rows, (r + 1) * rows), slice(span + r * rows, span + (r + 1) * rows)
        own_ref[r, :, HEAD_DIM : 2 * HEAD_DIM] = dk_all[later, :].astype(BF16)
        own_ref[r, :, 2 * HEAD_DIM : 3 * HEAD_DIM] = dv_all[later, :].astype(BF16)
        own_ref[r, :, 3 * HEAD_DIM :] = jnp.zeros((rows, own_ref.shape[2] - 3 * HEAD_DIM), BF16)
        back_ref[r, :, 0:HEAD_DIM] = dk_all[here, :].astype(BF16)
        back_ref[r, :, HEAD_DIM : 2 * HEAD_DIM] = dv_all[here, :].astype(BF16)
        back_ref[r, :, 2 * HEAD_DIM :] = jnp.zeros((rows, back_ref.shape[2] - 2 * HEAD_DIM), BF16)


def post_kernel(
    since_ref, step_ref, bias_ref, rate_ref, b_ref, c_ref, wt_ref, conv_ref, gate_ref, mix_ref, tail_ref,
    cols_ref, rowc_ref, through_ref, state_ref, own_ref, back_ref,
    ret_own, ret_back, gconv_ref, ggate_ref, gstep_ref, gin_ref, gout_ref, total_ref,
    mask_ref, xp_ref, mix_bias, pair_ref, dpair_ref, dpad_ref, z_ref, u_ref, db_ref, dc_ref, spread_ref,
    sums_ref, edge_ref, end_ref, spill_ref, coef_out, coef_all, red_out, red_a, red_mid, red_b, own_buf,
    sends, receives, locals_,
):
    group, place, groups = where_am_i()
    head, head_count = lax.axis_index("head"), lax.axis_size("head")
    rows, heads = step_ref.shape
    channels = conv_ref.shape[1]
    pairs = channels // LANES
    peers = [lax.rem(place + d, PLACES) for d in range(1, PLACES)]
    post = Post(sends, receives)
    partners = [shard(group, peer, groups) for peer in peers]
    partners += [shard(group + side, other, groups) for side in (1, -1) for other in range(PLACES)]
    partners += [shard(group + far, place, groups) for far in range(2, groups - 1)]
    head_peers = [{"head": lax.rem(head + d, head_count)} for d in range(1, head_count)]
    wait_partners = greet(partners + head_peers)
    keep_in = pltpu.make_async_copy(own_ref.at[place], own_buf, locals_.at[0])
    keep_in.start()
    wait_partners()
    bulk = []
    for r in [place] + peers:
        bulk.append(post.send(back_ref.at[r], ret_back.at[place], shard(group - 1, r, groups)))
    for peer in peers:
        bulk.append(post.send(own_ref.at[peer], ret_own.at[place], shard(group, peer, groups)))
    keep_in.wait()
    keep_out = pltpu.make_async_copy(own_buf, ret_own.at[place], locals_.at[1])
    keep_out.start()

    fill_masks(since_ref, mask_ref)
    i, j = causal(rows)
    since = since_ref[...]
    mix_bias[...] = jnp.where((i >= j) & ((i - j).astype(F32) <= since), 0.0, NEG_FILL)
    b_part, c_part = group_part(b_ref), group_part(c_ref)
    pair_ref[...] = dot(c_part, b_part, 1, 1)
    spread_ref[...] = spreader(heads, channels)
    for ref in (dpair_ref, z_ref, u_ref, db_ref, dc_ref, dpad_ref):
        ref[...] = jnp.zeros_like(ref)
    lower = lax.broadcasted_iota(jnp.int32, (rows, LANES), 1) < LANES // 2
    lane = lax.broadcasted_iota(jnp.int32, (rows, heads), 1)

    def mixer(n, carry):
        lanes = pl.ds(pl.multiple_of(n * LANES, LANES), LANES)
        cols = cols_ref[n]
        wt = wt_ref[:, lanes]
        size = pair_columns(cols, 1, lower)
        enter = pair_columns(cols, 2, lower)
        to_end = pair_columns(cols, 3, lower)
        pre = conv_pre(conv_ref[:, lanes], tail_ref[:, lanes], wt, mask_ref, xp_ref)
        sig_pre = jax.nn.sigmoid(pre)
        act = pre * sig_pre
        x_half = (act * size).astype(BF16)
        gate = gate_ref[:, lanes].astype(F32)
        sig_gate = jax.nn.sigmoid(gate)
        silu_gate = gate * sig_gate
        cot = mix_ref[:, lanes].astype(F32)
        dy = cot * silu_gate
        dy_half = dy.astype(BF16)
        state = jnp.concatenate([state_ref[r, 0, :, lanes] for r in range(PLACES)], axis=0)
        end_cot = jnp.concatenate([state_ref[r, 1, :, lanes] for r in range(PLACES)], axis=0)
        zero = jnp.zeros_like(dy_half)
        y_parts, dx_parts = [], []
        dpair = dpair_ref[...]
        rowc = rowc_ref[n]
        for k in range(2):
            weights = jnp.exp((cols[:, k : k + 1] - rowc[k : k + 1, :]) + mix_bias[...])
            mixing = (pair_ref[...] * weights).astype(BF16)
            y_parts.append(dot(mixing, x_half, 1, 0))
            dx_parts.append(dot(mixing, dy_half, 0, 0))
            dy_one = jnp.where(lower if k == 0 else ~lower, dy_half, zero)
            dpair = dpair + dot(dy_one, x_half, 1, 1) * weights
        dpair_ref[...] = dpair
        inner = jnp.where(lower, y_parts[0], y_parts[1]) + enter * dot(c_part, state, 1, 0)
        end_part = to_end * dot(b_part, end_cot, 1, 0)
        dx = jnp.where(lower, dx_parts[0], dx_parts[1]) + end_part
        skip = wt[KERNEL : KERNEL + 1, :]
        y = inner + skip * act
        ggate_ref[:, lanes] = (cot * y * (sig_gate + silu_gate * (1.0 - sig_gate))).astype(BF16)
        x_wide = x_half.astype(F32)
        zed = dy_half.astype(F32) * inner - x_wide * dx
        you = dx * act
        for k in range(2):
            side = lower if k == 0 else ~lower
            here = lane == 2 * n + k
            z_one = jnp.sum(jnp.where(side, zed, 0.0), axis=1, keepdims=True)
            u_one = jnp.sum(jnp.where(side, you, 0.0), axis=1, keepdims=True)
            z_ref[...] = jnp.where(here, z_one, z_ref[...])
            u_ref[...] = jnp.where(here, u_one, u_ref[...])
        dc_ref[...] += dot((enter * dy).astype(BF16), state, 1, 1)
        db_ref[...] += dot((to_end * x_wide).astype(BF16), end_cot, 1, 1)
        dact = dx * size + skip * dy
        dpre = dact * (sig_pre + act * (1.0 - sig_pre))
        sums_ref[0:1, lanes] = jnp.sum(dpre * xp_ref[PAD:, :], axis=0, keepdims=True)
        dpad_ref[0, PAD : PAD + rows, :] = dpre
        grown = wt[0:1, :] * dpad_ref[0, 0 : rows + PAD, :]
        for lag in range(1, KERNEL):
            masked = dpre * mask_ref[lag - 1]
            sums_ref[lag : lag + 1, lanes] = jnp.sum(
                masked * xp_ref[PAD - lag : PAD - lag + rows, :], axis=0, keepdims=True
            )
            dpad_ref[lag, PAD : PAD + rows, :] = masked
            grown = grown + wt[lag : lag + 1, :] * dpad_ref[lag, lag : lag + rows + PAD, :]
        gconv_ref[:, lanes] = grown[PAD:, :].astype(BF16)
        edge_ref[:, lanes] = grown[:PAD, :]
        end_ref[:, lanes] = grown[rows:, :]
        sums_ref[4:5, lanes] = jnp.sum(dy * act, axis=0, keepdims=True)
        sums_ref[5:6, lanes] = jnp.sum(state.astype(F32) * end_cot.astype(F32), axis=0, keepdims=True)
        sums_ref[6:7, lanes] = jnp.sum(x_wide * end_part, axis=0, keepdims=True)
        sums_ref[7:8, lanes] = jnp.zeros((1, LANES), F32)
        return carry

    lax.fori_loop(0, pairs, mixer, 0)

    first = place == 0
    former = shard(jnp.where(first, group - 1, group), lax.rem(place + PLACES - 1, PLACES), groups)
    spill_copy = post.send(edge_ref, spill_ref, former)
    raw = step_ref[...] + bias_ref[...]
    step = jnp.maximum(raw, 0.0) + jnp.log1p(jnp.exp(-jnp.abs(raw)))
    rate = jnp.exp(rate_ref[...])
    tri = (i >= j).astype(F32)
    per_head = dot(sums_ref[...], spread_ref[...], 1, 1, EXACT)[:, 0:heads]
    last_row = per_head[6:7] + through_ref[...] * per_head[5:6]
    t = lax.broadcasted_iota(jnp.int32, (rows, 1), 0)
    dcum = z_ref[...] + jnp.where(t == rows - 1, last_row, 0.0)
    dlog = dot(tri, dcum, 0, 0, EXACT)
    grad_step = (u_ref[...] - dlog * rate) * jax.nn.sigmoid(raw)
    gstep_ref[...] = grad_step
    red_out[...] = jnp.where(
        lax.broadcasted_iota(jnp.int32, red_out.shape, 0) < KERNEL, sums_ref[...], 0.0
    )
    red_out[4:5, 0:heads] = jnp.sum(grad_step, axis=0, keepdims=True)
    red_out[5:6, 0:heads] = jnp.sum(dlog * (-step * rate), axis=0, keepdims=True)
    red_out[6:7, 0:heads] = per_head[4:5]
    near = [post.send(red_out, red_a.at[place], shard(group, peer, groups)) for peer in peers]
    red_a[place] = red_out[...]
    dpair = dpair_ref[...]
    dc_ref[...] += dot(dpair, b_part.astype(F32), 1, 0, EXACT)
    db_ref[...] += dot(dpair, c_part.astype(F32), 0, 0, EXACT)
    coef_out[...] = jnp.concatenate([db_ref[...], dc_ref[...]], axis=1).astype(BF16)
    coefs = [post.send(coef_out, coef_all.at[head], peer) for peer in head_peers]
    coef_all[head] = coef_out[...]
    for copy in near:
        copy.wait()
    red_mid[...] = red_a[0] + red_a[1] + red_a[2] + red_a[3]
    wide = [
        post.send(red_mid, red_b.at[group], shard(group + far, place, groups)) for far in range(1, groups)
    ]
    red_b[group] = red_mid[...]
    spill_copy.wait()
    gconv_ref[rows - PAD :, :] = (end_ref[...] + spill_ref[...]).astype(BF16)
    for copy in coefs:
        copy.wait()
    halves = [coef_all[2 * n].astype(F32) + coef_all[2 * n + 1].astype(F32) for n in range(2)]
    half = coef_out.shape[1] // 2
    gin_ref[...] = jnp.concatenate([halves[0][:, :half], halves[1][:, :half]], axis=1)
    gout_ref[...] = jnp.concatenate([halves[0][:, half:], halves[1][:, half:]], axis=1)
    for copy in wide:
        copy.wait()
    total = red_b[0]
    for n in range(1, groups):
        total = total + red_b[n]
    total_ref[...] = total
    for copy in bulk:
        copy.wait()
    keep_out.wait()


def unpack_kernel(own_ref, back_ref, dq_ref, dk_ref, dv_ref):
    for r in range(own_ref.shape[0]):
        cols = slice(r * HEAD_DIM, (r + 1) * HEAD_DIM)
        dq_ref[:, cols] = own_ref[r, :, 0:HEAD_DIM]
        key = own_ref[r, :, HEAD_DIM : 2 * HEAD_DIM].astype(F32) + back_ref[r, :, 0:HEAD_DIM].astype(F32)
        dk_ref[:, cols] = (key * SCALE).astype(BF16)
        value = own_ref[r, :, 2 * HEAD_DIM : 3 * HEAD_DIM].astype(F32)
        dv_ref[:, cols] = (value + back_ref[r, :, HEAD_DIM : 2 * HEAD_DIM].astype(F32)).astype(BF16)


def local(
    queries, keys, values, attn_grad, doc_ids, conv_input, conv_weight, step_raw, step_bias,
    rate_log, skip_gain, input_coeff, output_coeff, gate_input, mix_grad,
):
    rows, width = queries.shape
    heads, channels = step_raw.shape[1], conv_input.shape[1]
    pairs = channels // LANES
    index = lax.axis_index("seq")
    groups = lax.axis_size("seq") // PLACES
    base = (index // PLACES) * PLACES * rows
    counts = jnp.sum(doc_ids[None, :] < jnp.arange(DOCS)[:, None], axis=1)
    docs = lax.dynamic_slice_in_dim(doc_ids, base, PLACES * rows)
    start = jnp.sum(jnp.where(docs[None, :] == jnp.arange(DOCS)[:, None], counts[:, None], 0), axis=0)
    where = base + jnp.arange(PLACES * rows, dtype=jnp.int32)
    low = (jnp.maximum(start, where - (WINDOW - 1)) - base + WINDOW).reshape(PLACES, rows)
    since = lax.dynamic_slice_in_dim(where - start, index % PLACES * rows, rows).astype(F32)[:, None]
    wt = jnp.concatenate(
        [conv_weight, jnp.repeat(skip_gain, channels // heads)[None], jnp.zeros((7 - KERNEL, channels), F32)]
    )
    bias, rate = step_bias[None], rate_log[None]

    struct = jax.ShapeDtypeStruct
    vmem = pl.BlockSpec(memory_space=pltpu.VMEM)
    loose = pl.BlockSpec(memory_space=pl.ANY)
    dma = lambda n: pltpu.SemaphoreType.DMA((n,))
    params = lambda n: pltpu.CompilerParams(
        collective_id=n, has_side_effects=True, vmem_limit_bytes=56 * 1024 * 1024
    )
    packed, key_cols = 4 * HEAD_DIM, 4 * LANES
    quarter = (2, 2 * PAD, channels)
    part = quarter[1:]
    recv, prev, cols, rowc, through, state, tail = pl.pallas_call(
        pre_kernel,
        in_specs=[vmem] * 11 + [loose] * 3,
        out_specs=[loose] * 2 + [vmem] * 5,
        out_shape=[
            struct((PLACES, rows, packed), BF16), struct((PLACES, rows, key_cols), BF16),
            struct((pairs, rows, 8), F32), struct((pairs, 2, rows), F32), struct((1, heads), F32),
            struct((PLACES, *quarter), BF16), struct((2 * PAD, channels), BF16),
        ],
        scratch_shapes=[
            pltpu.VMEM((PLACES, rows, packed), BF16),
            pltpu.VMEM((rows, channels), BF16), pltpu.VMEM((rows, channels), BF16),
            pltpu.VMEM((rows, channels), BF16), pltpu.VMEM((2 * PAD, channels), BF16),
            pltpu.VMEM((LANES, channels), F32), pltpu.VMEM((KERNEL - 1, rows, LANES), F32),
            pltpu.VMEM((rows + PAD, LANES), F32),
            pltpu.VMEM((PLACES, *quarter), BF16), pltpu.VMEM((PLACES, *quarter), BF16),
            pltpu.VMEM(part, BF16), pltpu.VMEM(part, BF16), pltpu.VMEM((PAD, LANES), F32),
            pltpu.VMEM((REACH, *part), BF16), pltpu.VMEM((REACH, *part), BF16),
            pltpu.VMEM((REACH, PAD, LANES), F32), pltpu.VMEM((REACH, PAD, LANES), F32),
            pltpu.VMEM((PLACES, *quarter), BF16), pltpu.VMEM((PLACES, *quarter), BF16),
            pltpu.VMEM((PAD, LANES), F32), pltpu.VMEM((PLACES, PAD, LANES), F32),
            dma(33), dma(33), dma(3), dma(1),
        ],
        name="pre",
        compiler_params=params(0),
    )(
        queries, keys, values, attn_grad, since, step_raw, bias, rate, input_coeff, output_coeff, wt,
        conv_input, gate_input, mix_grad,
    )
    span = PLACES * rows
    own, back = pl.pallas_call(
        attn_kernel,
        in_specs=[vmem] * 3,
        out_specs=[vmem] * 2,
        out_shape=[struct((PLACES, rows, 6 * LANES), BF16), struct((PLACES, rows, key_cols), BF16)],
        scratch_shapes=[
            pltpu.VMEM((span, HEAD_DIM), BF16), pltpu.VMEM((span, HEAD_DIM), BF16),
            pltpu.VMEM((2 * span, HEAD_DIM), BF16), pltpu.VMEM((2 * span, HEAD_DIM), BF16),
            pltpu.VMEM((2 * span, HEAD_DIM), F32), pltpu.VMEM((2 * span, HEAD_DIM), F32),
        ],
        name="attn",
        compiler_params=pltpu.CompilerParams(vmem_limit_bytes=56 * 1024 * 1024),
    )(low, recv, prev)
    wide_buf = lambda n: pltpu.VMEM((n, PAD, channels), F32)
    flat = pltpu.VMEM((PAD, channels), F32)
    ret_own, ret_back, gconv, ggate, gstep, gin, gout, total = pl.pallas_call(
        post_kernel,
        in_specs=[vmem] * 15 + [loose] * 2,
        out_specs=[loose] * 2 + [vmem] * 6,
        out_shape=[
            struct((PLACES, rows, 6 * LANES), BF16), struct((PLACES, rows, key_cols), BF16),
            struct((rows, channels), BF16), struct((rows, channels), BF16), struct((rows, heads), F32),
            struct((rows, LANES), F32), struct((rows, LANES), F32), struct((PAD, channels), F32),
        ],
        scratch_shapes=[
            pltpu.VMEM((KERNEL - 1, rows, LANES), F32), pltpu.VMEM((rows + PAD, LANES), F32),
            pltpu.VMEM((rows, rows), F32), pltpu.VMEM((rows, rows), F32), pltpu.VMEM((rows, rows), F32),
            pltpu.VMEM((KERNEL, rows + 2 * PAD, LANES), F32),
            pltpu.VMEM((rows, heads), F32), pltpu.VMEM((rows, heads), F32),
            pltpu.VMEM((rows, LANES // 2), F32), pltpu.VMEM((rows, LANES // 2), F32),
            pltpu.VMEM((LANES, channels), F32),
            flat, flat, flat, flat,
            pltpu.VMEM((rows, LANES), BF16), pltpu.VMEM((4, rows, LANES), BF16),
            flat, wide_buf(PLACES), flat, wide_buf(groups),
            pltpu.VMEM((rows, 6 * LANES), BF16),
            dma(21), dma(21), dma(2),
        ],
        name="post",
        compiler_params=params(1),
    )(
        since, step_raw, bias, rate, input_coeff, output_coeff, wt, conv_input, gate_input, mix_grad, tail,
        cols, rowc, through, state, own, back,
    )
    dq, dk, dv = pl.pallas_call(
        unpack_kernel,
        in_specs=[vmem] * 2,
        out_specs=[vmem] * 3,
        out_shape=[struct((rows, width), BF16)] * 3,
        name="unpack",
    )(ret_own, ret_back)
    return (
        dq, dk, dv, gconv, ggate, gstep, gin, gout, total[:KERNEL],
        total[4, :heads], total[5, :heads], total[6, :heads],
    )


def solution(mesh):
    sharded = P("seq", "head")
    return jax.shard_map(
        local,
        mesh=mesh,
        in_specs=(
            sharded, sharded, sharded, sharded, P(), sharded, P(None, "head"), sharded,
            P("head"), P("head"), P("head"), P("seq", None), P("seq", None), sharded, sharded,
        ),
        out_specs=(
            sharded, sharded, sharded, sharded, sharded, sharded,
            P("seq", None), P("seq", None), P(None, "head"), P("head"), P("head"), P("head"),
        ),
        check_vma=False,
    )
```

profile of v0, /device:TPU:0, one launch (start us, length us, event | category | flops | bytes accessed | tf_op | source)
XLA Modules:
  0.0 158.6 jit_solution(4447236312059060204)
XLA Ops:
  0.7 0.9 convert_reduce_fusion
  1.6 0.1 pad.2.clone
  1.7 0.7 dynamic_slice.6
  2.4 0.1 select_reduce_fusion
  2.5 0.1 dynamic-slice_convert_fusion
  2.6 0.6 subtract_add_fusion.low_ref
  3.2 0.7 broadcast_in_dim.37
  3.9 0.1 broadcast_in_dim_reshape.3
  4.0 1.4 maximum_maximum_fusion.wt_ref
  5.4 0.8 copy.37.since_ref
  6.2 1.5 copy.38.step_ref
  7.7 74.8 %pre.1 = (bf16[4,256,896]{2,1,0:T(8,128)(2,1)}, bf16[4,256,512]{2,1,0:T(8,128)(2,1)}, f32[14,256,8]{2,1,0:T(8,128)}, f32[14,2,256]{2,1,0:T(2,128)}, f32[1,28]{1,...) custom-call(bf16[256,896]{1,0:T(8,128)(2,1)} %q_ref.1, bf16[256,896]{1,0:T(8,128)(2,1)} %k_ref.1, ...), custom_call_target="tpu_custom_call" | custom-call | tf_op jit(solution)/shard_map/pre/pallas_call | solution.py:526
  82.5 12.5 %attn.1 = (bf16[4,256,768]{2,1,0:T(8,128)(2,1)}, bf16[4,256,512]{2,1,0:T(8,128)(2,1)}) custom-call(s32[4,256]{1,0:T(4,128)} %subtract_add_fusion.low_ref, bf16[4,256,896]{2,1,0:T(8,128)(2,1)} %get-tuple-element.37.recv_ref, bf16[4,256,512]{2,1,0:T(8,128)(2,1)} %get-tuple-element.38.prev_ref), custom_call_target="tpu_custom_call" | custom-call | tf_op jit(solution)/shard_map/attn/pallas_call | solution.py:556
  95.1 54.7 %post.1 = (bf16[4,256,768]{2,1,0:T(8,128)(2,1)}, bf16[4,256,512]{2,1,0:T(8,128)(2,1)}, bf16[256,1792]{1,0:T(8,128)(2,1)}, bf16[256,1792]{1,0:T(8,128)(2,1)}, f32...) custom-call(f32[256,1]{1,0:T(8,128)} %copy.37.since_ref, ...), custom_call_target="tpu_custom_call" | custom-call | tf_op jit(solution)/shard_map/post/pallas_call | solution.py:571
  149.8 0.0 copy-start.5
  149.8 0.0 copy-start.2
  149.8 0.0 copy-start.1
  149.8 0.0 copy-start
  149.8 3.8 %unpack.1 = (bf16[256,896]{1,0:T(8,128)(2,1)}, bf16[256,896]{1,0:T(8,128)(2,1)}, bf16[256,896]{1,0:T(8,128)(2,1)}) custom-call(bf16[4,256,768]{2,1,0:T(8,128)(2,1)} %get-tuple-element.41.own_ref, bf16[4,256,512]{2,1,0:T(8,128)(2,1)} %get-tuple-element.42.back_ref), custom_call_target="tpu_custom_call" | custom-call | tf_op jit(solution)/shard_map/unpack/pallas_call | solution.py:599
  153.6 0.0 copy-done.5
  153.6 0.5 slice_bitcast_fusion
  154.1 0.6 slice.12
  154.7 0.0 copy-done.2
  154.7 0.7 copy.39
  155.4 0.0 copy-done.1
  155.4 0.0 copy-start.4
  155.4 0.0 copy-start.3
  155.4 0.9 copy.44
  156.4 0.0 copy-done
  156.4 0.9 copy.45
  157.3 0.0 copy-done.4
  157.3 0.7 copy.46
  157.9 0.0 copy-done.3
  157.9 0.7 copy.47
  (3 shorter events, 0.0 us)
Async XLA Ops:
  149.8 3.8 %copy-start.5 = (f32[8,1792]{1,0:T(8,128)S(1)}, f32[8,1792]{1,0:T(8,128)}, u32[]{:S(2)}) copy-start(f32[8,1792]{1,0:T(8,128)} %get-tuple-element.51) | copy-start | bytes 172036
  149.8 4.9 %copy-start.2 = (f32[256,28]{1,0:T(8,128)S(1)}, f32[256,28]{1,0:T(8,128)}, u32[]{:S(2)}) copy-start(f32[256,28]{1,0:T(8,128)} %get-tuple-element.81) | copy-start | bytes 86020
  149.8 5.6 %copy-start.1 = (bf16[256,1792]{1,0:T(8,128)(2,1)S(1)}, bf16[256,1792]{1,0:T(8,128)(2,1)}, u32[]{:S(2)}) copy-start(bf16[256,1792]{1,0:T(8,128)(2,1)} %get-tuple-element.106) | copy-start | bytes 2752516
  149.8 6.5 %copy-start = (bf16[256,1792]{1,0:T(8,128)(2,1)S(1)}, bf16[256,1792]{1,0:T(8,128)(2,1)}, u32[]{:S(2)}) copy-start(bf16[256,1792]{1,0:T(8,128)(2,1)} %get-tuple-element.107) | copy-start | bytes 2752516
  155.4 1.9 %copy-start.4 = (f32[256,128]{1,0:T(8,128)S(1)}, f32[256,128]{1,0:T(8,128)}, u32[]{:S(2)}) copy-start(f32[256,128]{1,0:T(8,128)} %get-tuple-element.109) | copy-start | bytes 393220
  155.4 2.5 %copy-start.3 = (f32[256,128]{1,0:T(8,128)S(1)}, f32[256,128]{1,0:T(8,128)}, u32[]{:S(2)}) copy-start(f32[256,128]{1,0:T(8,128)} %get-tuple-element.110) | copy-start | bytes 393220
where the time goes:
time: 159 us
  Pallas kernels  146 us (92%)
  local copies, waits for them, and re-layouts  8.91 us (6%)
  other arithmetic  3.15 us (2%)
    pallas_call x1, Pallas kernels, local(): pl.pallas_call(pre_kernel, in_specs=[vmem] * 11 + [loose] * 3, out_specs=...  74.8 us
    pallas_call x1, Pallas kernels, local(): pl.pallas_call(post_kernel, in_specs=[vmem] * 15 + [loose] * 2, out_specs...  54.7 us
    pallas_call x1, Pallas kernels, local(): pl.pallas_call(attn_kernel, in_specs=[vmem] * 3, out_specs=[vmem] * 2, ou...  12.5 us
    unnamed x18, local copies, waits for them, and re-layouts  5.4 us
    pallas_call x1, Pallas kernels, local(): pl.pallas_call(unpack_kernel, in_specs=[vmem] * 2, out_specs=[vmem] * 3,...  3.75 us

commit v1 on v0

v1 whole, which is shorter than its diff:
```python
import jax
import jax.numpy as jnp
from jax import lax
from jax.experimental import pallas as pl
from jax.experimental.pallas import tpu as pltpu
from jax.sharding import PartitionSpec as P

HEAD_DIM = 224
WINDOW = 1024
KERNEL = 4
PAD = 8
LANES = 128
PLACES = 4
DOCS = 8
REACH = 4

EXACT = lax.Precision.HIGHEST
F32 = jnp.float32
BF16 = jnp.bfloat16
NEG_FILL = -1e30
SENDS = 56
SCALE = HEAD_DIM ** (-0.5)


def dot(a, b, ca, cb, precision=None):
    return lax.dot_general(
        a, b, (((ca,), (cb,)), ((), ())), preferred_element_type=F32, precision=precision
    )


def where_am_i():
    index = lax.axis_index("seq")
    groups = lax.axis_size("seq") // PLACES
    return lax.div(index, PLACES), lax.rem(index, PLACES), groups


def shard(group, place, groups):
    return {"seq": lax.rem(group + 2 * groups, groups) * PLACES + place}


def greet(partners):
    barrier = pltpu.get_barrier_semaphore()
    for partner in partners:
        pl.semaphore_signal(barrier, inc=1, device_id=partner, device_id_type=pl.DeviceIdType.MESH)
    return lambda: pl.semaphore_wait(barrier, len(partners))


class Post:
    def __init__(self, sends, receives):
        self.sends, self.receives, self.used = sends, receives, 0

    def send(self, source, target, device):
        copy = pltpu.make_async_remote_copy(
            src_ref=source, dst_ref=target, send_sem=self.sends.at[self.used],
            recv_sem=self.receives.at[self.used], device_id=device,
            device_id_type=pl.DeviceIdType.MESH,
        )
        self.used += 1
        copy.start()
        return copy


def spreader(heads, channels):
    width = channels // heads
    row = lax.broadcasted_iota(jnp.int32, (LANES, channels), 0)
    col = lax.broadcasted_iota(jnp.int32, (LANES, channels), 1)
    return ((col >= row * width) & (col < row * width + width)).astype(F32)


def causal(rows):
    i = lax.broadcasted_iota(jnp.int32, (rows, rows), 0)
    j = lax.broadcasted_iota(jnp.int32, (rows, rows), 1)
    return i, j


def pair_columns(cols, index, lower):
    return jnp.where(lower, cols[:, 2 * index : 2 * index + 1], cols[:, 2 * index + 1 : 2 * index + 2])


def fill_masks(since_ref, mask_ref):
    for lag in range(1, KERNEL):
        mask_ref[lag - 1] = jnp.broadcast_to((since_ref[...] >= lag).astype(F32), mask_ref.shape[1:])


def conv_pre(conv, tail, wt, mask_ref, xp_ref):
    rows = conv.shape[0]
    xp_ref[:PAD, :] = tail.astype(F32)[PAD:]
    xp_ref[PAD:, :] = conv.astype(F32)
    pre = wt[0:1, :] * xp_ref[PAD:, :]
    for lag in range(1, KERNEL):
        pre = pre + wt[lag : lag + 1, :] * (xp_ref[PAD - lag : PAD - lag + rows, :] * mask_ref[lag - 1])
    return pre


def group_part(ref):
    half = ref.shape[1] // 2
    whole = ref[...].astype(F32)
    first = lax.axis_index("head") < lax.axis_size("head") // 2
    return jnp.where(first, whole[:, :half], whole[:, half:]).astype(BF16)


def whole_kernel(
    since_ref, low_ref, step_ref, bias_ref, rate_ref, b_ref, c_ref, wt_ref,
    k_hbm, v_hbm, q_hbm, do_hbm, conv_hbm, gate_hbm, mix_hbm,
    dq_ref, dk_ref, dv_ref, gconv_ref, ggate_ref, gstep_ref, gin_ref, gout_ref, total_ref,
    k_ref, v_ref, q_ref, do_ref, conv_ref, gate_ref, mix_ref,
    pack_ref, recv_ref, prev_ref, q_all, do_all, k_all, v_all, dk_all, dv_all,
    back_out, back_in, dq_out, dq_in, kv_out, kv_in,
    tail_buf, cols_ref, rowc_ref, spread_ref, mask_ref, xp_ref,
    ends_ref, a_ref, end_out, cot_out, g_out, e_in, c_in, ge_in, gc_in, chain_out, state_ref, t_out, t_all,
    mix_bias, pair_ref, dpair_ref, dpad_ref, z_ref, u_ref, db_ref, dc_ref,
    sums_ref, edge_ref, end_ref, spill_ref, coef_out, coef_all, red_out, red_a, red_mid, red_b,
    sends, receives, back_sends, back_receives, loads,
):
    group, place, groups = where_am_i()
    head, head_count = lax.axis_index("head"), lax.axis_size("head")
    rows, heads = step_ref.shape
    channels = conv_ref.shape[1]
    pairs = channels // LANES
    span = PLACES * rows
    peers = [lax.rem(place + d, PLACES) for d in range(1, PLACES)]
    post = Post(sends, receives)
    fetches = []
    for n, (source, target) in enumerate((
        (k_hbm, k_ref), (v_hbm, v_ref), (q_hbm, q_ref), (do_hbm, do_ref),
        (conv_hbm, conv_ref), (gate_hbm, gate_ref), (mix_hbm, mix_ref),
    )):
        fetches.append(pltpu.make_async_copy(source, target, loads.at[n]))
        fetches[-1].start()
    partners = [shard(group + far, place, groups) for far in range(1, groups)]
    partners += [shard(group, peer, groups) for peer in peers]
    last, first = place == PLACES - 1, place == 0
    follower = shard(jnp.where(last, group + 1, group), lax.rem(place + 1, PLACES), groups)
    former = shard(jnp.where(first, group - 1, group), lax.rem(place + PLACES - 1, PLACES), groups)
    head_peers = [{"head": lax.rem(head + d, head_count)} for d in range(1, head_count)]
    wait_partners = greet(partners + [follower, former] + head_peers)

    for n, ref in ((2, k_ref), (3, v_ref), (1, do_ref), (0, q_ref)):
        fetches[(2, 3, 0, 1)[n]].wait()
        for r in range(PLACES):
            pack_ref[r, :, n * HEAD_DIM : (n + 1) * HEAD_DIM] = ref[:, r * HEAD_DIM : (r + 1) * HEAD_DIM]
    fetches[4].wait()
    wait_partners()
    ahead = shard(group + 1, place, groups)
    behind = shard(group - 1, place, groups)
    tail_copy = post.send(conv_ref.at[rows - 2 * PAD :, :], tail_buf, follower)
    key_cols, other_cols = pl.ds(3 * LANES, 4 * LANES), pl.ds(0, 3 * LANES)
    near_keys = [
        post.send(pack_ref.at[peer, :, key_cols], recv_ref.at[place, :, key_cols], shard(group, peer, groups))
        for peer in peers
    ]
    far_keys = [post.send(pack_ref.at[place, :, key_cols], prev_ref.at[place], ahead)]
    near_others = [
        post.send(pack_ref.at[peer, :, other_cols], recv_ref.at[place, :, other_cols], shard(group, peer, groups))
        for peer in peers
    ]
    recv_ref[place] = pack_ref[place]

    since = since_ref[...]
    raw = step_ref[...] + bias_ref[...]
    step = jnp.maximum(raw, 0.0) + jnp.log1p(jnp.exp(-jnp.abs(raw)))
    rate = jnp.exp(rate_ref[...])
    log_decay = -step * rate
    i, j = causal(rows)
    tri = (i >= j).astype(F32)
    cum = dot(tri, log_decay, 1, 0, EXACT)
    row_cum = dot(log_decay, tri, 0, 1, EXACT)
    t = lax.broadcasted_iota(jnp.int32, (rows, 1), 0)
    enter = jnp.where(since > t.astype(F32), jnp.exp(cum), 0.0)
    final = cum[rows - 1 : rows]
    to_end = jnp.where((rows - 1 - t).astype(F32) <= since[rows - 1 : rows], jnp.exp(final - cum), 0.0)
    through = enter[rows - 1 : rows]
    t_out[...] = jnp.zeros_like(t_out)
    t_out[0:1, 0:heads] = through
    t_all[place] = t_out[...]
    t_copies = [post.send(t_out, t_all.at[place], shard(group, peer, groups)) for peer in peers]
    for n in range(pairs):
        two = slice(2 * n, 2 * n + 2)
        cols_ref[n] = jnp.concatenate([cum[:, two], step[:, two], enter[:, two], to_end[:, two]], axis=1)
        rowc_ref[n] = row_cum[two]
    spread_ref[...] = spreader(heads, channels)
    fill_masks(since_ref, mask_ref)
    lower = lax.broadcasted_iota(jnp.int32, (rows, LANES), 1) < LANES // 2
    b_part, c_part = group_part(b_ref), group_part(c_ref)
    fetches[5].wait()
    fetches[6].wait()
    tail_copy.wait()

    def ends(n, carry):
        lanes = pl.ds(pl.multiple_of(n * LANES, LANES), LANES)
        cols = cols_ref[n]
        pre = conv_pre(conv_ref[:, lanes], tail_buf[:, lanes], wt_ref[:, lanes], mask_ref, xp_ref)
        act = pre * jax.nn.sigmoid(pre)
        weighted = act * pair_columns(cols, 1, lower) * pair_columns(cols, 3, lower)
        end = dot(b_part, weighted.astype(BF16), 0, 0).astype(BF16)
        gate = gate_ref[:, lanes].astype(F32)
        dy = mix_ref[:, lanes].astype(F32) * (gate * jax.nn.sigmoid(gate))
        start = dot(c_part, (dy * pair_columns(cols, 2, lower)).astype(BF16), 0, 0).astype(BF16)
        for r in range(PLACES):
            part = slice(2 * PAD * r, 2 * PAD * (r + 1))
            ends_ref[r, 0, :, lanes] = end[part]
            ends_ref[r, 1, :, lanes] = start[part]
        return carry

    lax.fori_loop(0, pairs // 2, ends, 0)
    for d in range(1, PLACES):
        near_keys[d - 1].wait()
        source = lax.rem(place + PLACES - d, PLACES)
        far_keys.append(post.send(recv_ref.at[source, :, key_cols], prev_ref.at[source], ahead))
    lax.fori_loop(pairs // 2, pairs, ends, 0)

    a_copies = [post.send(ends_ref.at[peer], a_ref.at[place], shard(group, peer, groups)) for peer in peers]
    a_ref[place] = ends_ref[place]
    for copy in near_others:
        copy.wait()
    for r in range(PLACES):
        here, later = slice(r * rows, (r + 1) * rows), slice(span + r * rows, span + (r + 1) * rows)
        q_all[here, :] = recv_ref[r, :, 0:HEAD_DIM]
        do_all[here, :] = recv_ref[r, :, HEAD_DIM : 2 * HEAD_DIM]
        k_all[later, :] = recv_ref[r, :, 2 * HEAD_DIM : 3 * HEAD_DIM]
        v_all[later, :] = recv_ref[r, :, 3 * HEAD_DIM : 4 * HEAD_DIM]
    dk_all[...] = jnp.zeros_like(dk_all)
    dv_all[...] = jnp.zeros_like(dv_all)
    for copy in t_copies + a_copies:
        copy.wait()
    decays = dot(t_all[...].reshape(PLACES * PAD, LANES), spread_ref[...], 1, 0, EXACT)
    decay = [decays[PAD * n : PAD * n + 1] for n in range(PLACES)]
    end_of = lambda n: a_ref[n, 0].astype(F32)
    cot_of = lambda n: a_ref[n, 1].astype(F32)
    end, cot = end_of(0), cot_of(PLACES - 1)
    for n in range(1, PLACES):
        end = end_of(n) + decay[n] * end
        cot = cot_of(PLACES - 1 - n) + decay[PLACES - 1 - n] * cot
    end_out[...] = end.astype(BF16)
    cot_out[...] = cot.astype(BF16)
    g_out[...] = t_all[0] * t_all[1] * t_all[2] * t_all[3]
    b_copies = []
    for far in range(1, REACH + 1):
        later, earlier = shard(group + far, place, groups), shard(group - far, place, groups)
        b_copies.append(post.send(g_out, ge_in.at[far - 1], later))
        b_copies.append(post.send(g_out, gc_in.at[far - 1], earlier))
        b_copies.append(post.send(end_out, e_in.at[far - 1], later))
        b_copies.append(post.send(cot_out, c_in.at[far - 1], earlier))
    for copy in b_copies:
        copy.wait()
    before = dot(ge_in[...].reshape(REACH * PAD, LANES), spread_ref[...], 1, 0, EXACT)
    after = dot(gc_in[...].reshape(REACH * PAD, LANES), spread_ref[...], 1, 0, EXACT)
    state = e_in[REACH - 1].astype(F32)
    cot = c_in[REACH - 1].astype(F32) * (group + REACH < groups).astype(F32)
    for far in range(REACH - 2, -1, -1):
        state = e_in[far].astype(F32) + before[PAD * far : PAD * far + 1] * state
        cot = (c_in[far].astype(F32) + after[PAD * far : PAD * far + 1] * cot) * (
            group + far + 1 < groups
        ).astype(F32)
    for n in range(PLACES):
        chain_out[n, 0] = state.astype(BF16)
        state = end_of(n) + decay[n] * state
        m = PLACES - 1 - n
        chain_out[m, 1] = cot.astype(BF16)
        cot = cot_of(m) + decay[m] * cot
    state_copies = [
        post.send(chain_out.at[peer], state_ref.at[place], shard(group, peer, groups)) for peer in peers
    ]
    state_ref[place] = chain_out[place]

    for copy in far_keys:
        copy.wait()
    skip = 2 * HEAD_DIM - 3 * LANES
    for r in range(PLACES):
        here = slice(r * rows, (r + 1) * rows)
        k_all[here, :] = prev_ref[r, :, skip : skip + HEAD_DIM]
        v_all[here, :] = prev_ref[r, :, skip + HEAD_DIM : skip + 2 * HEAD_DIM]

    def back_copy(b):
        return pltpu.make_async_remote_copy(
            src_ref=back_out.at[b], dst_ref=back_in.at[b], send_sem=back_sends.at[b],
            recv_sem=back_receives.at[b], device_id=behind, device_id_type=pl.DeviceIdType.MESH,
        )

    def block(b, carry):
        mine = pl.ds(pl.multiple_of(b * rows, rows), rows)
        q = q_all[mine, :]
        grad = do_all[mine, :]
        low = low_ref[pl.ds(b, 1), :]
        at = [pl.ds(pl.multiple_of((b + PLACES - gap) * rows, rows), rows) for gap in range(PLACES + 1)]
        scores = []
        top = None
        for gap in range(PLACES + 1):
            allowed = i + (b + PLACES - gap) * rows >= low
            if gap == 0:
                allowed = allowed & (j >= i)
            s = jnp.where(allowed, dot(k_all[at[gap], :], q, 1, 1) * SCALE, NEG_FILL)
            scores.append(s)
            m = jnp.max(s, axis=0, keepdims=True)
            top = m if top is None else jnp.maximum(top, m)
        total = None
        expo = []
        for gap in range(PLACES + 1):
            e = jnp.exp(scores[gap] - top)
            expo.append(e)
            e_sum = jnp.sum(e, axis=0, keepdims=True)
            total = e_sum if total is None else total + e_sum
        inverse = 1.0 / jnp.maximum(total, 1.0)
        delta = None
        dprobs = []
        for gap in range(PLACES + 1):
            half = (expo[gap] * inverse).astype(BF16)
            dp = dot(v_all[at[gap], :], grad, 1, 1)
            d = jnp.sum(half.astype(F32) * dp, axis=0, keepdims=True)
            delta = d if delta is None else delta + d
            dv_all[at[gap], :] += dot(half, grad, 1, 0)
            dprobs.append(dp)
        dq = None
        for gap in range(PLACES + 1):
            ds = (expo[gap] * inverse * (dprobs[gap] - delta)).astype(BF16)
            dk_all[at[gap], :] += dot(ds, q, 1, 0)
            part = dot(ds, k_all[at[gap], :], 0, 0)
            dq = part if dq is None else dq + part
        dq_out[b, :, 0:HEAD_DIM] = (dq * SCALE).astype(BF16)
        back_out[b, :, 0:HEAD_DIM] = dk_all[mine, :].astype(BF16)
        back_out[b, :, HEAD_DIM : 2 * HEAD_DIM] = dv_all[mine, :].astype(BF16)
        back_copy(b).start()
        return carry

    lax.fori_loop(0, PLACES, block, 0)
    dq_copies = [post.send(dq_out.at[peer], dq_in.at[place], shard(group, peer, groups)) for peer in peers]
    dq_in[place] = dq_out[place]

    mix_bias[...] = jnp.where((i >= j) & ((i - j).astype(F32) <= since), 0.0, NEG_FILL)
    pair_ref[...] = dot(c_part, b_part, 1, 1)
    for ref in (dpair_ref, z_ref, u_ref, db_ref, dc_ref, dpad_ref):
        ref[...] = jnp.zeros_like(ref)
    lane = lax.broadcasted_iota(jnp.int32, (rows, heads), 1)
    for copy in state_copies:
        copy.wait()

    def mixer(n, carry):
        lanes = pl.ds(pl.multiple_of(n * LANES, LANES), LANES)
        cols = cols_ref[n]
        wt = wt_ref[:, lanes]
        size = pair_columns(cols, 1, lower)
        enter = pair_columns(cols, 2, lower)
        to_end = pair_columns(cols, 3, lower)
        pre = conv_pre(conv_ref[:, lanes], tail_buf[:, lanes], wt, mask_ref, xp_ref)
        sig_pre = jax.nn.sigmoid(pre)
        act = pre * sig_pre
        x_half = (act * size).astype(BF16)
        gate = gate_ref[:, lanes].astype(F32)
        sig_gate = jax.nn.sigmoid(gate)
        silu_gate = gate * sig_gate
        cot = mix_ref[:, lanes].astype(F32)
        dy = cot * silu_gate
        dy_half = dy.astype(BF16)
        state = jnp.concatenate([state_ref[r, 0, :, lanes] for r in range(PLACES)], axis=0)
        end_cot = jnp.concatenate([state_ref[r, 1, :, lanes] for r in range(PLACES)], axis=0)
        zero = jnp.zeros_like(dy_half)
        y_parts, dx_parts = [], []
        dpair = dpair_ref[...]
        rowc = rowc_ref[n]
        for k in range(2):
            weights = jnp.exp((cols[:, k : k + 1] - rowc[k : k + 1, :]) + mix_bias[...])
            mixing = (pair_ref[...] * weights).astype(BF16)
            y_parts.append(dot(mixing, x_half, 1, 0))
            dx_parts.append(dot(mixing, dy_half, 0, 0))
            dy_one = jnp.where(lower if k == 0 else ~lower, dy_half, zero)
            dpair = dpair + dot(dy_one, x_half, 1, 1) * weights
        dpair_ref[...] = dpair
        inner = jnp.where(lower, y_parts[0], y_parts[1]) + enter * dot(c_part, state, 1, 0)
        end_part = to_end * dot(b_part, end_cot, 1, 0)
        dx = jnp.where(lower, dx_parts[0], dx_parts[1]) + end_part
        skip = wt[KERNEL : KERNEL + 1, :]
        y = inner + skip * act
        ggate_ref[:, lanes] = (cot * y * (sig_gate + silu_gate * (1.0 - sig_gate))).astype(BF16)
        x_wide = x_half.astype(F32)
        zed = dy_half.astype(F32) * inner - x_wide * dx
        you = dx * act
        for k in range(2):
            side = lower if k == 0 else ~lower
            here = lane == 2 * n + k
            z_one = jnp.sum(jnp.where(side, zed, 0.0), axis=1, keepdims=True)
            u_one = jnp.sum(jnp.where(side, you, 0.0), axis=1, keepdims=True)
            z_ref[...] = jnp.where(here, z_one, z_ref[...])
            u_ref[...] = jnp.where(here, u_one, u_ref[...])
        dc_ref[...] += dot((enter * dy).astype(BF16), state, 1, 1)
        db_ref[...] += dot((to_end * x_wide).astype(BF16), end_cot, 1, 1)
        dact = dx * size + skip * dy
        dpre = dact * (sig_pre + act * (1.0 - sig_pre))
        sums_ref[0:1, lanes] = jnp.sum(dpre * xp_ref[PAD:, :], axis=0, keepdims=True)
        dpad_ref[0, PAD : PAD + rows, :] = dpre
        grown = wt[0:1, :] * dpad_ref[0, 0 : rows + PAD, :]
        for lag in range(1, KERNEL):
            masked = dpre * mask_ref[lag - 1]
            sums_ref[lag : lag + 1, lanes] = jnp.sum(
                masked * xp_ref[PAD - lag : PAD - lag + rows, :], axis=0, keepdims=True
            )
            dpad_ref[lag, PAD : PAD + rows, :] = masked
            grown = grown + wt[lag : lag + 1, :] * dpad_ref[lag, lag : lag + rows + PAD, :]
        gconv_ref[:, lanes] = grown[PAD:, :].astype(BF16)
        edge_ref[:, lanes] = grown[:PAD, :]
        end_ref[:, lanes] = grown[rows:, :]
        sums_ref[4:5, lanes] = jnp.sum(dy * act, axis=0, keepdims=True)
        sums_ref[5:6, lanes] = jnp.sum(state.astype(F32) * end_cot.astype(F32), axis=0, keepdims=True)
        sums_ref[6:7, lanes] = jnp.sum(x_wide * end_part, axis=0, keepdims=True)
        sums_ref[7:8, lanes] = jnp.zeros((1, LANES), F32)
        return carry

    lax.fori_loop(0, pairs // 2, mixer, 0)
    for b in range(PLACES):
        back_copy(b).wait()
        rear = slice(span + b * rows, span + (b + 1) * rows)
        key = dk_all[rear, :] + back_in[b, :, 0:HEAD_DIM].astype(F32)
        kv_out[b, :, 0:HEAD_DIM] = (key * SCALE).astype(BF16)
        value = dv_all[rear, :] + back_in[b, :, HEAD_DIM : 2 * HEAD_DIM].astype(F32)
        kv_out[b, :, HEAD_DIM : 2 * HEAD_DIM] = value.astype(BF16)
    kv_copies = [post.send(kv_out.at[peer], kv_in.at[place], shard(group, peer, groups)) for peer in peers]
    kv_in[place] = kv_out[place]
    lax.fori_loop(pairs // 2, pairs, mixer, 0)

    spill_copy = post.send(edge_ref, spill_ref, former)
    per_head = dot(sums_ref[...], spread_ref[...], 1, 1, EXACT)[:, 0:heads]
    last_row = per_head[6:7] + through * per_head[5:6]
    dcum = z_ref[...] + jnp.where(t == rows - 1, last_row, 0.0)
    dlog = dot(tri, dcum, 0, 0, EXACT)
    grad_step = (u_ref[...] - dlog * rate) * jax.nn.sigmoid(raw)
    gstep_ref[...] = grad_step
    red_out[...] = jnp.where(
        lax.broadcasted_iota(jnp.int32, red_out.shape, 0) < KERNEL, sums_ref[...], 0.0
    )
    red_out[4:5, 0:heads] = jnp.sum(grad_step, axis=0, keepdims=True)
    red_out[5:6, 0:heads] = jnp.sum(dlog * log_decay, axis=0, keepdims=True)
    red_out[6:7, 0:heads] = per_head[4:5]
    near = [post.send(red_out, red_a.at[place], shard(group, peer, groups)) for peer in peers]
    red_a[place] = red_out[...]
    dpair = dpair_ref[...]
    dc_ref[...] += dot(dpair, b_part.astype(F32), 1, 0, EXACT)
    db_ref[...] += dot(dpair, c_part.astype(F32), 0, 0, EXACT)
    coef_out[...] = jnp.concatenate([db_ref[...], dc_ref[...]], axis=1).astype(BF16)
    coefs = [post.send(coef_out, coef_all.at[head], peer) for peer in head_peers]
    coef_all[head] = coef_out[...]
    for copy in near:
        copy.wait()
    red_mid[...] = red_a[0] + red_a[1] + red_a[2] + red_a[3]
    wide = [
        post.send(red_mid, red_b.at[group], shard(group + far, place, groups)) for far in range(1, groups)
    ]
    red_b[group] = red_mid[...]
    spill_copy.wait()
    gconv_ref[rows - PAD :, :] = (end_ref[...] + spill_ref[...]).astype(BF16)
    for copy in coefs:
        copy.wait()
    halves = [coef_all[2 * n].astype(F32) + coef_all[2 * n + 1].astype(F32) for n in range(2)]
    half = coef_out.shape[1] // 2
    gin_ref[...] = jnp.concatenate([halves[0][:, :half], halves[1][:, :half]], axis=1)
    gout_ref[...] = jnp.concatenate([halves[0][:, half:], halves[1][:, half:]], axis=1)
    for copy in dq_copies + kv_copies:
        copy.wait()
    for r in range(PLACES):
        cols = slice(r * HEAD_DIM, (r + 1) * HEAD_DIM)
        dq_ref[:, cols] = dq_in[r, :, 0:HEAD_DIM]
        dk_ref[:, cols] = kv_in[r, :, 0:HEAD_DIM]
        dv_ref[:, cols] = kv_in[r, :, HEAD_DIM : 2 * HEAD_DIM]
    for copy in wide:
        copy.wait()
    total = red_b[0]
    for n in range(1, groups):
        total = total + red_b[n]
    total_ref[...] = total


def local(
    queries, keys, values, attn_grad, doc_ids, conv_input, conv_weight, step_raw, step_bias,
    rate_log, skip_gain, input_coeff, output_coeff, gate_input, mix_grad,
):
    rows, width = queries.shape
    heads, channels = step_raw.shape[1], conv_input.shape[1]
    pairs = channels // LANES
    index = lax.axis_index("seq")
    groups = lax.axis_size("seq") // PLACES
    base = (index // PLACES) * PLACES * rows
    counts = jnp.sum(doc_ids[None, :] < jnp.arange(DOCS)[:, None], axis=1)
    docs = lax.dynamic_slice_in_dim(doc_ids, base, PLACES * rows)
    start = jnp.sum(jnp.where(docs[None, :] == jnp.arange(DOCS)[:, None], counts[:, None], 0), axis=0)
    where = base + jnp.arange(PLACES * rows, dtype=jnp.int32)
    low = (jnp.maximum(start, where - (WINDOW - 1)) - base + WINDOW).reshape(PLACES, rows)
    since = lax.dynamic_slice_in_dim(where - start, index % PLACES * rows, rows).astype(F32)[:, None]
    wt = jnp.concatenate(
        [conv_weight, jnp.repeat(skip_gain, channels // heads)[None], jnp.zeros((7 - KERNEL, channels), F32)]
    )
    bias, rate = step_bias[None], rate_log[None]

    struct = jax.ShapeDtypeStruct
    vmem = pl.BlockSpec(memory_space=pltpu.VMEM)
    loose = pl.BlockSpec(memory_space=pl.ANY)
    dma = lambda n: pltpu.SemaphoreType.DMA((n,))
    params = lambda n: pltpu.CompilerParams(
        collective_id=n, has_side_effects=True, vmem_limit_bytes=56 * 1024 * 1024
    )
    packed, keys_wide = 4 * HEAD_DIM, 4 * LANES
    quarter = (2, 2 * PAD, channels)
    part = quarter[1:]
    span = PLACES * rows
    half = lambda *shape: pltpu.VMEM(shape, BF16)
    full = lambda *shape: pltpu.VMEM(shape, F32)
    flat = full(PAD, channels)
    outs = pl.pallas_call(
        whole_kernel,
        in_specs=[vmem] * 8 + [loose] * 7,
        out_specs=[vmem] * 9,
        out_shape=[
            struct((rows, width), BF16), struct((rows, width), BF16), struct((rows, width), BF16),
            struct((rows, channels), BF16), struct((rows, channels), BF16), struct((rows, heads), F32),
            struct((rows, LANES), F32), struct((rows, LANES), F32), struct((PAD, channels), F32),
        ],
        scratch_shapes=[
            half(rows, width), half(rows, width), half(rows, width), half(rows, width),
            half(rows, channels), half(rows, channels), half(rows, channels),
            half(PLACES, rows, packed), half(PLACES, rows, packed), half(PLACES, rows, keys_wide),
            half(span, HEAD_DIM), half(span, HEAD_DIM), half(2 * span, HEAD_DIM), half(2 * span, HEAD_DIM),
            full(2 * span, HEAD_DIM), full(2 * span, HEAD_DIM),
            half(PLACES, rows, keys_wide), half(PLACES, rows, keys_wide),
            half(PLACES, rows, 2 * LANES), half(PLACES, rows, 2 * LANES),
            half(PLACES, rows, keys_wide), half(PLACES, rows, keys_wide),
            half(2 * PAD, channels), full(pairs, rows, 8), full(pairs, 2, rows), full(LANES, channels),
            full(KERNEL - 1, rows, LANES), full(rows + PAD, LANES),
            half(PLACES, *quarter), half(PLACES, *quarter), half(*part), half(*part), full(PAD, LANES),
            half(REACH, *part), half(REACH, *part), full(REACH, PAD, LANES), full(REACH, PAD, LANES),
            half(PLACES, *quarter), half(PLACES, *quarter), full(PAD, LANES), full(PLACES, PAD, LANES),
            full(rows, rows), full(rows, rows), full(rows, rows), full(KERNEL, rows + 2 * PAD, LANES),
            full(rows, heads), full(rows, heads), full(rows, LANES // 2), full(rows, LANES // 2),
            flat, flat, flat, flat, half(rows, LANES), half(4, rows, LANES),
            flat, full(PLACES, PAD, channels), flat, full(groups, PAD, channels),
            dma(SENDS), dma(SENDS), dma(PLACES), dma(PLACES), dma(7),
        ],
        name="whole",
        compiler_params=params(0),
    )(
        since, low, step_raw, bias, rate, input_coeff, output_coeff, wt,
        keys, values, queries, attn_grad, conv_input, gate_input, mix_grad,
    )
    total = outs[-1]
    return (
        *outs[:-1], total[:KERNEL], total[4, :heads], total[5, :heads], total[6, :heads],
    )


def solution(mesh):
    sharded = P("seq", "head")
    return jax.shard_map(
        local,
        mesh=mesh,
        in_specs=(
            sharded, sharded, sharded, sharded, P(), sharded, P(None, "head"), sharded,
            P("head"), P("head"), P("head"), P("seq", None), P("seq", None), sharded, sharded,
        ),
        out_specs=(
            sharded, sharded, sharded, sharded, sharded, sharded,
            P("seq", None), P("seq", None), P(None, "head"), P("head"), P("head"), P("head"),
        ),
        check_vma=False,
    )
```

time: 159 us -> 118 us (0.74)
  Pallas kernels: 146 us -> 100 us
  local copies, waits for them, and re-layouts: 8.91 us -> 15.2 us
    pallas_call x4 -> x1, Pallas kernels: 146 us -> 100 us  [local(): pl.pallas_call(whole_kernel, in_specs=[vmem] * 8 + [loose] * 7, out_specs...]
    unnamed x18 -> x29, local copies, waits for them, and re-layouts: 5.4 us -> 10.7 us
where the time goes in v1:
time: 118 us
  Pallas kernels  100 us (85%)
  local copies, waits for them, and re-layouts  15.2 us (13%)
  other arithmetic  1.64 us (1%)
    pallas_call x1, Pallas kernels, local(): pl.pallas_call(whole_kernel, in_specs=[vmem] * 8 + [loose] * 7, out_specs...  100 us
    unnamed x29, local copies, waits for them, and re-layouts  10.7 us

profile of v1, /device:TPU:0, one launch (start us, length us, event | category | flops | bytes accessed | tf_op | source)
XLA Modules:
  0.0 117.5 jit_solution(8986269117730371013)
XLA Ops:
  0.6 0.0 copy-start.6
  0.7 0.7 copy-done.6
  1.4 0.2 convert_reduce_fusion
  1.6 0.1 pad.2.clone
  1.7 0.0 dynamic-slice-start
  1.7 0.7 dynamic-slice-done
  2.4 0.1 select_reduce_fusion
  2.4 0.0 copy-start.9
  2.5 0.0 copy-start.8
  2.5 0.1 dynamic-slice_convert_fusion
  2.6 0.6 subtract_add_fusion.low_ref
  3.2 0.0 copy-done.9
  3.2 0.1 broadcast_in_dim.37
  3.2 0.1 broadcast_in_dim_reshape.3
  3.3 0.0 copy-done.8
  3.3 0.7 maximum_maximum_fusion.wt_ref
  4.0 0.0 copy-start.7
  4.0 0.8 copy.32.since_ref
  4.8 0.0 copy-done.7
  4.8 0.8 copy.33.step_ref
  5.6 100.0 %whole.1 = (bf16[256,896]{1,0:T(8,128)(2,1)}, bf16[256,896]{1,0:T(8,128)(2,1)}, bf16[256,896]{1,0:T(8,128)(2,1)}, bf16[256,1792]{1,0:T(8,128)(2,1)}, bf16[256,17...) custom-call(f32[256,1]{1,0:T(8,128)} %copy.32.since_ref, ...), custom_call_target="tpu_custom_call" | custom-call | tf_op jit(solution)/shard_map/whole/pallas_call | solution.py:505
  105.6 1.3 %slice_bitcast_fusion = (f32[28]{0:T(128)}, f32[28]{0:T(128)}, f32[28]{0:T(128)}) fusion(f32[8,1792]{1,0:T(8,128)} %get-tuple-element.29), kind=kLoop, calls=%fused_computation.8 | loop fusion | bytes 672 | tf_op jit(solution)/shard_map/squeeze | solution.py:542
  106.9 1.4 %slice.12 = f32[4,1792]{1,0:T(4,128)} slice(f32[8,1792]{1,0:T(8,128)} %get-tuple-element.29), slice={[0:4], [0:1792]} | slice | bytes 57344 | tf_op jit(solution)/shard_map/slice | solution.py:542
  108.3 1.6 %copy.34 = f32[256,28]{0,1:T(8,128)} copy(f32[256,28]{1,0:T(8,128)} %get-tuple-element.59) | data formatting | bytes 57344
  109.9 0.0 copy-start.3
  109.9 0.0 copy-start.2
  109.9 1.9 %copy.42 = bf16[256,896]{1,0:T(8,128)(2,1)} copy(bf16[256,896]{1,0:T(8,128)(2,1)} %get-tuple-element.81) | data formatting | bytes 917504
  111.8 0.0 copy-done.3
  111.8 0.0 copy-start.1
  111.8 0.8 copy.43
  112.6 0.0 copy-done.2
  112.6 0.8 copy.44
  113.4 0.0 copy-done.1
  113.4 0.0 copy-start
  113.4 0.9 copy.45
  114.3 0.6 copy-done
  114.9 0.0 copy-start.5
  114.9 0.9 copy.46
  115.8 0.1 copy-done.5
  115.9 0.0 copy-start.4
  115.9 0.7 copy.47
  116.6 0.3 copy-done.4
  116.9 0.7 copy.48
  (3 shorter events, 0.0 us)
Async XLA Ops:
  0.6 0.8 copy-start.6
  1.7 0.7 dynamic-slice-start
  2.4 0.7 copy-start.9
  2.5 0.9 copy-start.8
  4.0 0.8 copy-start.7
  109.9 1.9 %copy-start.3 = (bf16[256,896]{1,0:T(8,128)(2,1)S(1)}, bf16[256,896]{1,0:T(8,128)(2,1)}, u32[]{:S(2)}) copy-start(bf16[256,896]{1,0:T(8,128)(2,1)} %get-tuple-element.82) | copy-start | bytes 1376260
  109.9 2.7 %copy-start.2 = (bf16[256,896]{1,0:T(8,128)(2,1)S(1)}, bf16[256,896]{1,0:T(8,128)(2,1)}, u32[]{:S(2)}) copy-start(bf16[256,896]{1,0:T(8,128)(2,1)} %get-tuple-element.83) | copy-start | bytes 1376260
  111.8 1.5 %copy-start.1 = (bf16[256,1792]{1,0:T(8,128)(2,1)S(1)}, bf16[256,1792]{1,0:T(8,128)(2,1)}, u32[]{:S(2)}) copy-start(bf16[256,1792]{1,0:T(8,128)(2,1)} %get-tuple-element.84) | copy-start | bytes 2752516
  113.4 1.5 %copy-start = (bf16[256,1792]{1,0:T(8,128)(2,1)S(1)}, bf16[256,1792]{1,0:T(8,128)(2,1)}, u32[]{:S(2)}) copy-start(bf16[256,1792]{1,0:T(8,128)(2,1)} %get-tuple-element.85) | copy-start | bytes 2752516
  114.9 1.0 copy-start.5
  115.9 1.0 copy-start.4

commit v2 on v1

v2 whole, which is shorter than its diff:
```python
import jax
import jax.numpy as jnp
from jax import lax
from jax.experimental import pallas as pl
from jax.experimental.pallas import tpu as pltpu
from jax.sharding import PartitionSpec as P

HEAD_DIM = 224
WINDOW = 1024
KERNEL = 4
PAD = 8
LANES = 128
PLACES = 4
DOCS = 8
REACH = 4

EXACT = lax.Precision.HIGHEST
F32 = jnp.float32
BF16 = jnp.bfloat16
NEG_FILL = -1e30
SENDS = 69
SCALE = HEAD_DIM ** (-0.5)


def dot(a, b, ca, cb, precision=None):
    return lax.dot_general(
        a, b, (((ca,), (cb,)), ((), ())), preferred_element_type=F32, precision=precision
    )


def where_am_i():
    index = lax.axis_index("seq")
    groups = lax.axis_size("seq") // PLACES
    return lax.div(index, PLACES), lax.rem(index, PLACES), groups


def shard(group, place, groups):
    return {"seq": lax.rem(group + 2 * groups, groups) * PLACES + place}


def greet(partners):
    barrier = pltpu.get_barrier_semaphore()
    for partner in partners:
        pl.semaphore_signal(barrier, inc=1, device_id=partner, device_id_type=pl.DeviceIdType.MESH)
    return lambda: pl.semaphore_wait(barrier, len(partners))


class Post:
    def __init__(self, sends, receives):
        self.sends, self.receives, self.used = sends, receives, 0

    def send(self, source, target, device):
        copy = pltpu.make_async_remote_copy(
            src_ref=source, dst_ref=target, send_sem=self.sends.at[self.used],
            recv_sem=self.receives.at[self.used], device_id=device,
            device_id_type=pl.DeviceIdType.MESH,
        )
        self.used += 1
        copy.start()
        return copy


def spreader(heads, channels):
    width = channels // heads
    row = lax.broadcasted_iota(jnp.int32, (LANES, channels), 0)
    col = lax.broadcasted_iota(jnp.int32, (LANES, channels), 1)
    return ((col >= row * width) & (col < row * width + width)).astype(F32)


def causal(rows):
    i = lax.broadcasted_iota(jnp.int32, (rows, rows), 0)
    j = lax.broadcasted_iota(jnp.int32, (rows, rows), 1)
    return i, j


def pair_columns(cols, index, lower):
    return jnp.where(lower, cols[:, 2 * index : 2 * index + 1], cols[:, 2 * index + 1 : 2 * index + 2])


def fill_masks(since_ref, mask_ref):
    for lag in range(1, KERNEL):
        mask_ref[lag - 1] = jnp.broadcast_to((since_ref[...] >= lag).astype(F32), mask_ref.shape[1:])


def conv_pre(conv, tail, wt, mask_ref, xp_ref):
    rows = conv.shape[0]
    xp_ref[:PAD, :] = tail.astype(F32)[PAD:]
    xp_ref[PAD:, :] = conv.astype(F32)
    pre = wt[0:1, :] * xp_ref[PAD:, :]
    for lag in range(1, KERNEL):
        pre = pre + wt[lag : lag + 1, :] * (xp_ref[PAD - lag : PAD - lag + rows, :] * mask_ref[lag - 1])
    return pre


def group_part(ref):
    half = ref.shape[1] // 2
    whole = ref[...].astype(F32)
    first = lax.axis_index("head") < lax.axis_size("head") // 2
    return jnp.where(first, whole[:, :half], whole[:, half:]).astype(BF16)


def whole_kernel(
    since_ref, low_ref, step_ref, bias_ref, rate_ref, skip_ref, b_ref, c_ref, weight_ref,
    k_hbm, v_hbm, q_hbm, do_hbm, conv_hbm, gate_hbm, mix_hbm,
    dq_in, dk_in, dv_in, gconv_ref, ggate_ref, gfix_ref, gstep_ref, gin_ref, gout_ref, total_ref,
    k_ref, v_ref, q_ref, do_ref, conv_ref, gate_ref, mix_ref,
    k_pack, v_pack, q_pack, do_pack, q_all, do_all, k_all, v_all, dk_all, dv_all,
    dk_out, dv_out, dk_back, dv_back, dq_own, dk_own, dv_own,
    tail_buf, wt_ref, cols_ref, rowc_ref, spread_ref, mask_ref, xp_ref,
    act_all, slope_all, dy_all, cg_all, inner_all, dx_all,
    ends_ref, a_ref, end_out, cot_out, g_out, e_in, c_in, ge_in, gc_in, chain_out, state_ref, t_out, t_all,
    mix_bias, pair_ref, dpair_ref, dpad_ref, z_ref, u_ref, db_ref, dc_ref,
    sums_ref, edge_ref, end_ref, spill_ref, coef_out, coef_all, red_out, red_a, red_mid, red_b,
    sends, receives, back_sends, back_receives, loads, keeps,
):
    group, place, groups = where_am_i()
    head, head_count = lax.axis_index("head"), lax.axis_size("head")
    rows, heads = step_ref.shape
    channels = conv_ref.shape[1]
    pairs = channels // LANES
    peers = [lax.rem(place + d, PLACES) for d in range(1, PLACES)]
    post = Post(sends, receives)
    fetches = []
    for n, (source, target) in enumerate((
        (k_hbm, k_ref), (v_hbm, v_ref), (conv_hbm, conv_ref), (q_hbm, q_ref), (do_hbm, do_ref),
        (gate_hbm, gate_ref), (mix_hbm, mix_ref),
    )):
        fetches.append(pltpu.make_async_copy(source, target, loads.at[n]))
        fetches[-1].start()
    partners = [shard(group + far, place, groups) for far in range(1, groups)]
    partners += [shard(group, peer, groups) for peer in peers]
    last, first = place == PLACES - 1, place == 0
    follower = shard(jnp.where(last, group + 1, group), lax.rem(place + 1, PLACES), groups)
    former = shard(jnp.where(first, group - 1, group), lax.rem(place + PLACES - 1, PLACES), groups)
    head_peers = [{"head": lax.rem(head + d, head_count)} for d in range(1, head_count)]
    wait_partners = greet(partners + [follower, former] + head_peers)
    ahead = shard(group + 1, place, groups)
    behind = shard(group - 1, place, groups)

    def pack(source, target):
        for r in range(PLACES):
            target[r, :, 0:HEAD_DIM] = source[:, r * HEAD_DIM : (r + 1) * HEAD_DIM]
            target[r, :, HEAD_DIM:] = jnp.zeros((rows, target.shape[2] - HEAD_DIM), BF16)

    def spread(source, target, offset):
        return [
            post.send(source.at[peer], target.at[offset + place], shard(group, peer, groups)) for peer in peers
        ]

    fetches[0].wait()
    pack(k_ref, k_pack)
    fetches[1].wait()
    pack(v_ref, v_pack)
    fetches[2].wait()
    wait_partners()
    tail_copy = post.send(conv_ref.at[rows - 2 * PAD :, :], tail_buf, follower)
    far = [post.send(k_pack.at[place], k_all.at[place], ahead)]
    near_k = spread(k_pack, k_all, PLACES)
    far.append(post.send(v_pack.at[place], v_all.at[place], ahead))
    near_v = spread(v_pack, v_all, PLACES)
    fetches[3].wait()
    pack(q_ref, q_pack)
    fetches[4].wait()
    pack(do_ref, do_pack)
    near = spread(q_pack, q_all, 0) + spread(do_pack, do_all, 0)

    since = since_ref[...]
    raw = step_ref[...] + bias_ref[...]
    step = jnp.maximum(raw, 0.0) + jnp.log1p(jnp.exp(-jnp.abs(raw)))
    rate = jnp.exp(rate_ref[...])
    log_decay = -step * rate
    i, j = causal(rows)
    tri = (i >= j).astype(F32)
    cum = dot(tri, log_decay, 1, 0, EXACT)
    row_cum = dot(log_decay, tri, 0, 1, EXACT)
    t = lax.broadcasted_iota(jnp.int32, (rows, 1), 0)
    enter = jnp.where(since > t.astype(F32), jnp.exp(cum), 0.0)
    final = cum[rows - 1 : rows]
    to_end = jnp.where((rows - 1 - t).astype(F32) <= since[rows - 1 : rows], jnp.exp(final - cum), 0.0)
    through = enter[rows - 1 : rows]
    t_out[...] = jnp.zeros_like(t_out)
    t_out[0:1, 0:heads] = through
    t_all[place] = t_out[...]
    t_copies = [post.send(t_out, t_all.at[place], shard(group, peer, groups)) for peer in peers]
    for n in range(pairs):
        two = slice(2 * n, 2 * n + 2)
        cols_ref[n] = jnp.concatenate([cum[:, two], step[:, two], enter[:, two], to_end[:, two]], axis=1)
        rowc_ref[n] = row_cum[two]
    spread_ref[...] = spreader(heads, channels)
    wt_ref[0:KERNEL, :] = weight_ref[...]
    wt_ref[KERNEL : KERNEL + 1, :] = dot(skip_ref[...], spread_ref[0:heads, :], 1, 0, EXACT)
    fill_masks(since_ref, mask_ref)
    lower = lax.broadcasted_iota(jnp.int32, (rows, LANES), 1) < LANES // 2
    b_part, c_part = group_part(b_ref), group_part(c_ref)
    fetches[5].wait()
    fetches[6].wait()
    tail_copy.wait()

    def ends(n, carry):
        lanes = pl.ds(pl.multiple_of(n * LANES, LANES), LANES)
        cols = cols_ref[n]
        pre = conv_pre(conv_ref[:, lanes], tail_buf[:, lanes], wt_ref[:, lanes], mask_ref, xp_ref)
        sig_pre = jax.nn.sigmoid(pre)
        act = pre * sig_pre
        act_all[:, lanes] = act
        slope_all[:, lanes] = sig_pre + act * (1.0 - sig_pre)
        weighted = act * pair_columns(cols, 1, lower) * pair_columns(cols, 3, lower)
        end = dot(b_part, weighted.astype(BF16), 0, 0).astype(BF16)
        gate = gate_ref[:, lanes].astype(F32)
        sig_gate = jax.nn.sigmoid(gate)
        silu_gate = gate * sig_gate
        cot = mix_ref[:, lanes].astype(F32)
        dy = cot * silu_gate
        dy_all[:, lanes] = dy
        cg_all[:, lanes] = cot * (sig_gate + silu_gate * (1.0 - sig_gate))
        start = dot(c_part, (dy * pair_columns(cols, 2, lower)).astype(BF16), 0, 0).astype(BF16)
        for r in range(PLACES):
            part = slice(2 * PAD * r, 2 * PAD * (r + 1))
            ends_ref[r, 0, :, lanes] = end[part]
            ends_ref[r, 1, :, lanes] = start[part]
        return carry

    def pass_on(copies, target):
        for d in range(1, PLACES):
            copies[d - 1].wait()
            source = lax.rem(place + PLACES - d, PLACES)
            far.append(post.send(target.at[PLACES + source], target.at[source], ahead))

    lax.fori_loop(0, pairs // 4, ends, 0)
    pass_on(near_k, k_all)
    lax.fori_loop(pairs // 4, 3 * pairs // 4, ends, 0)
    pass_on(near_v, v_all)
    lax.fori_loop(3 * pairs // 4, pairs, ends, 0)

    a_copies = [post.send(ends_ref.at[peer], a_ref.at[place], shard(group, peer, groups)) for peer in peers]
    a_ref[place] = ends_ref[place]
    for mine, everyone, offset in (
        (k_pack, k_all, PLACES), (v_pack, v_all, PLACES), (q_pack, q_all, 0), (do_pack, do_all, 0)
    ):
        everyone[offset + place] = mine[place]
    dk_all[...] = jnp.zeros_like(dk_all)
    dv_all[...] = jnp.zeros_like(dv_all)

    mix_bias[...] = jnp.where((i >= j) & ((i - j).astype(F32) <= since), 0.0, NEG_FILL)
    pair_ref[...] = dot(c_part, b_part, 1, 1)
    for ref in (dpair_ref, z_ref, u_ref, db_ref, dc_ref, dpad_ref, red_out):
        ref[...] = jnp.zeros_like(ref)

    def within(n, carry):
        lanes = pl.ds(pl.multiple_of(n * LANES, LANES), LANES)
        cols = cols_ref[n]
        x_half = (act_all[:, lanes] * pair_columns(cols, 1, lower)).astype(BF16)
        dy_half = dy_all[:, lanes].astype(BF16)
        zero = jnp.zeros_like(dy_half)
        y_parts, dx_parts = [], []
        dpair = dpair_ref[...]
        rowc = rowc_ref[n]
        for k in range(2):
            weights = jnp.exp((cols[:, k : k + 1] - rowc[k : k + 1, :]) + mix_bias[...])
            mixing = (pair_ref[...] * weights).astype(BF16)
            y_parts.append(dot(mixing, x_half, 1, 0))
            dx_parts.append(dot(mixing, dy_half, 0, 0))
            dy_one = jnp.where(lower if k == 0 else ~lower, dy_half, zero)
            dpair = dpair + dot(dy_one, x_half, 1, 1) * weights
        dpair_ref[...] = dpair
        inner_all[:, lanes] = jnp.where(lower, y_parts[0], y_parts[1])
        dx_all[:, lanes] = jnp.where(lower, dx_parts[0], dx_parts[1])
        return carry

    lax.fori_loop(0, pairs // 3, within, 0)
    for copy in t_copies + a_copies:
        copy.wait()
    decays = dot(t_all[...].reshape(PLACES * PAD, LANES), spread_ref[...], 1, 0, EXACT)
    decay = [decays[PAD * n : PAD * n + 1] for n in range(PLACES)]
    end_of = lambda n: a_ref[n, 0].astype(F32)
    cot_of = lambda n: a_ref[n, 1].astype(F32)
    end, cot = end_of(0), cot_of(PLACES - 1)
    for n in range(1, PLACES):
        end = end_of(n) + decay[n] * end
        cot = cot_of(PLACES - 1 - n) + decay[PLACES - 1 - n] * cot
    end_out[...] = end.astype(BF16)
    cot_out[...] = cot.astype(BF16)
    g_out[...] = t_all[0] * t_all[1] * t_all[2] * t_all[3]
    b_copies = []
    for away in range(1, REACH + 1):
        later, earlier = shard(group + away, place, groups), shard(group - away, place, groups)
        b_copies.append(post.send(g_out, ge_in.at[away - 1], later))
        b_copies.append(post.send(g_out, gc_in.at[away - 1], earlier))
        b_copies.append(post.send(end_out, e_in.at[away - 1], later))
        b_copies.append(post.send(cot_out, c_in.at[away - 1], earlier))
    lax.fori_loop(pairs // 3, pairs, within, 0)
    for copy in b_copies:
        copy.wait()
    before = dot(ge_in[...].reshape(REACH * PAD, LANES), spread_ref[...], 1, 0, EXACT)
    after = dot(gc_in[...].reshape(REACH * PAD, LANES), spread_ref[...], 1, 0, EXACT)
    state = e_in[REACH - 1].astype(F32)
    cot = c_in[REACH - 1].astype(F32) * (group + REACH < groups).astype(F32)
    for away in range(REACH - 2, -1, -1):
        state = e_in[away].astype(F32) + before[PAD * away : PAD * away + 1] * state
        cot = (c_in[away].astype(F32) + after[PAD * away : PAD * away + 1] * cot) * (
            group + away + 1 < groups
        ).astype(F32)
    for n in range(PLACES):
        chain_out[n, 0] = state.astype(BF16)
        state = end_of(n) + decay[n] * state
        m = PLACES - 1 - n
        chain_out[m, 1] = cot.astype(BF16)
        cot = cot_of(m) + decay[m] * cot
    state_copies = [
        post.send(chain_out.at[peer], state_ref.at[place], shard(group, peer, groups)) for peer in peers
    ]
    state_ref[place] = chain_out[place]

    for copy in near + far:
        copy.wait()

    def back_copy(source, target, b, n):
        return pltpu.make_async_remote_copy(
            src_ref=source.at[b], dst_ref=target.at[b], send_sem=back_sends.at[n],
            recv_sem=back_receives.at[n], device_id=behind, device_id_type=pl.DeviceIdType.MESH,
        )

    def block(b, carry):
        q = q_all[b]
        grad = do_all[b]
        low = low_ref[pl.ds(b, 1), :]
        at = [b + PLACES - gap for gap in range(PLACES + 1)]
        scores = []
        top = None
        for gap in range(PLACES + 1):
            allowed = i + at[gap] * rows >= low
            if gap == 0:
                allowed = allowed & (j >= i)
            s = jnp.where(allowed, dot(k_all[at[gap]], q, 1, 1) * SCALE, NEG_FILL)
            scores.append(s)
            m = jnp.max(s, axis=0, keepdims=True)
            top = m if top is None else jnp.maximum(top, m)
        total = None
        expo = []
        for gap in range(PLACES + 1):
            e = jnp.exp(scores[gap] - top)
            expo.append(e)
            e_sum = jnp.sum(e, axis=0, keepdims=True)
            total = e_sum if total is None else total + e_sum
        inverse = 1.0 / jnp.maximum(total, 1.0)
        delta = None
        dprobs = []
        for gap in range(PLACES + 1):
            half = (expo[gap] * inverse).astype(BF16)
            dp = dot(v_all[at[gap]], grad, 1, 1)
            d = jnp.sum(half.astype(F32) * dp, axis=0, keepdims=True)
            delta = d if delta is None else delta + d
            dv_all[at[gap]] += dot(half, grad, 1, 0)
            dprobs.append(dp)
        dq = None
        for gap in range(PLACES + 1):
            ds = (expo[gap] * inverse * (dprobs[gap] - delta)).astype(BF16)
            dk_all[at[gap]] += dot(ds, q, 1, 0)
            part = dot(ds, k_all[at[gap]], 0, 0)
            dq = part if dq is None else dq + part
        dq_own[b] = (dq * SCALE).astype(BF16)
        dk_out[b] = dk_all[b].astype(BF16)
        dv_out[b] = dv_all[b].astype(BF16)
        back_copy(dk_out, dk_back, b, b).start()
        return carry

    lax.fori_loop(0, PLACES, block, 0)
    for b in range(PLACES):
        back_copy(dv_out, dv_back, b, PLACES + b).start()
    kept = []

    def give_back(source, target):
        copies = spread(source, target, 0)
        copies.append(pltpu.make_async_copy(source.at[place], target.at[place], keeps.at[len(kept)]))
        copies[-1].start()
        kept.extend(copies)

    give_back(dq_own, dq_in)

    def across(n, carry):
        lanes = pl.ds(pl.multiple_of(n * LANES, LANES), LANES)
        cols = cols_ref[n]
        wt = wt_ref[:, lanes]
        size = pair_columns(cols, 1, lower)
        enter = pair_columns(cols, 2, lower)
        to_end = pair_columns(cols, 3, lower)
        xp_ref[:PAD, :] = tail_buf[:, lanes].astype(F32)[PAD:]
        xp_ref[PAD:, :] = conv_ref[:, lanes].astype(F32)
        act = act_all[:, lanes]
        dy = dy_all[:, lanes]
        x_wide = (act * size).astype(BF16).astype(F32)
        state = jnp.concatenate([state_ref[r, 0, :, lanes] for r in range(PLACES)], axis=0)
        end_cot = jnp.concatenate([state_ref[r, 1, :, lanes] for r in range(PLACES)], axis=0)
        inner = inner_all[:, lanes] + enter * dot(c_part, state, 1, 0)
        end_part = to_end * dot(b_part, end_cot, 1, 0)
        dx = dx_all[:, lanes] + end_part
        skip = wt[KERNEL : KERNEL + 1, :]
        ggate_ref[:, lanes] = (cg_all[:, lanes] * (inner + skip * act)).astype(BF16)
        zed = dy.astype(BF16).astype(F32) * inner - x_wide * dx
        you = dx * act
        for k in range(2):
            side = lower if k == 0 else ~lower
            here = lane == 2 * n + k
            z_one = jnp.sum(jnp.where(side, zed, 0.0), axis=1, keepdims=True)
            u_one = jnp.sum(jnp.where(side, you, 0.0), axis=1, keepdims=True)
            z_ref[...] = jnp.where(here, z_one, z_ref[...])
            u_ref[...] = jnp.where(here, u_one, u_ref[...])
        dc_ref[...] += dot((enter * dy).astype(BF16), state, 1, 1)
        db_ref[...] += dot((to_end * x_wide).astype(BF16), end_cot, 1, 1)
        dpre = (dx * size + skip * dy) * slope_all[:, lanes]
        red_out[pl.ds(n, 1), :] = jnp.sum(dpre * xp_ref[PAD:, :], axis=0, keepdims=True)
        dpad_ref[0, PAD : PAD + rows, :] = dpre
        grown = wt[0:1, :] * dpad_ref[0, 0 : rows + PAD, :]
        for lag in range(1, KERNEL):
            masked = dpre * mask_ref[lag - 1]
            red_out[pl.ds(lag * pairs + n, 1), :] = jnp.sum(
                masked * xp_ref[PAD - lag : PAD - lag + rows, :], axis=0, keepdims=True
            )
            dpad_ref[lag, PAD : PAD + rows, :] = masked
            grown = grown + wt[lag : lag + 1, :] * dpad_ref[lag, lag : lag + rows + PAD, :]
        gconv_ref[:, lanes] = grown[PAD:, :].astype(BF16)
        edge_ref[:, lanes] = grown[:PAD, :]
        end_ref[:, lanes] = grown[rows:, :]
        sums_ref[0:1, lanes] = jnp.sum(dy * act, axis=0, keepdims=True)
        sums_ref[1:2, lanes] = jnp.sum(state.astype(F32) * end_cot.astype(F32), axis=0, keepdims=True)
        sums_ref[2:3, lanes] = jnp.sum(x_wide * end_part, axis=0, keepdims=True)
        sums_ref[3:8, lanes] = jnp.zeros((5, LANES), F32)
        return carry

    def whole_sum(source, target, total, out, offset, factor):
        for b in range(PLACES):
            back_copy(source, target, b, offset + b).wait()
            out[b] = ((total[PLACES + b] + target[b].astype(F32)) * factor).astype(BF16)

    lane = lax.broadcasted_iota(jnp.int32, (rows, heads), 1)
    for copy in state_copies:
        copy.wait()
    lax.fori_loop(0, pairs // 2, across, 0)
    whole_sum(dk_out, dk_back, dk_all, dk_own, 0, SCALE)
    give_back(dk_own, dk_in)
    lax.fori_loop(pairs // 2, pairs, across, 0)

    spill_copy = post.send(edge_ref, spill_ref, former)
    per_head = dot(sums_ref[...], spread_ref[...], 1, 1, EXACT)[:, 0:heads]
    last_row = per_head[2:3] + through * per_head[1:2]
    dcum = z_ref[...] + jnp.where(t == rows - 1, last_row, 0.0)
    dlog = dot(tri, dcum, 0, 0, EXACT)
    grad_step = (u_ref[...] - dlog * rate) * jax.nn.sigmoid(raw)
    gstep_ref[...] = grad_step
    small = KERNEL * pairs
    red_out[small : small + 1, 0:heads] = jnp.sum(grad_step, axis=0, keepdims=True)
    red_out[small + 1 : small + 2, 0:heads] = jnp.sum(dlog * log_decay, axis=0, keepdims=True)
    red_out[small + 2 : small + 3, 0:heads] = per_head[0:1]
    reds = [post.send(red_out, red_a.at[place], shard(group, peer, groups)) for peer in peers]
    red_a[place] = red_out[...]
    dpair = dpair_ref[...]
    dc_ref[...] += dot(dpair, b_part.astype(F32), 1, 0, EXACT)
    db_ref[...] += dot(dpair, c_part.astype(F32), 0, 0, EXACT)
    coef_out[...] = jnp.concatenate([db_ref[...], dc_ref[...]], axis=1).astype(BF16)
    coefs = [post.send(coef_out, coef_all.at[head], peer) for peer in head_peers]
    coef_all[head] = coef_out[...]
    for copy in reds:
        copy.wait()
    red_mid[...] = red_a[0] + red_a[1] + red_a[2] + red_a[3]
    wide = [
        post.send(red_mid, red_b.at[group], shard(group + away, place, groups)) for away in range(1, groups)
    ]
    red_b[group] = red_mid[...]
    whole_sum(dv_out, dv_back, dv_all, dv_own, PLACES, 1.0)
    give_back(dv_own, dv_in)
    spill_copy.wait()
    gfix_ref[...] = end_ref[...] + spill_ref[...]
    for copy in coefs:
        copy.wait()
    halves = [coef_all[2 * n].astype(F32) + coef_all[2 * n + 1].astype(F32) for n in range(2)]
    half = coef_out.shape[1] // 2
    gin_ref[...] = jnp.concatenate([halves[0][:, :half], halves[1][:, :half]], axis=1)
    gout_ref[...] = jnp.concatenate([halves[0][:, half:], halves[1][:, half:]], axis=1)
    for copy in wide:
        copy.wait()
    total = red_b[0]
    for n in range(1, groups):
        total = total + red_b[n]
    total_ref[...] = total
    for copy in kept:
        copy.wait()


def finish_kernel(
    dq_in, dk_in, dv_in, gconv_in, ggate_in, gfix_ref, gstep_in, gin_in, gout_in, total_ref,
    dq_ref, dk_ref, dv_ref, gconv_ref, ggate_ref, gstep_ref, gin_ref, gout_ref, conv_ref, bias_ref, rate_ref, skip_ref,
):
    for source, target in ((dq_in, dq_ref), (dk_in, dk_ref), (dv_in, dv_ref)):
        for r in range(PLACES):
            target[:, r * HEAD_DIM : (r + 1) * HEAD_DIM] = source[r, :, 0:HEAD_DIM]
    for source, target in (
        (gconv_in, gconv_ref), (ggate_in, ggate_ref), (gstep_in, gstep_ref), (gin_in, gin_ref), (gout_in, gout_ref)
    ):
        target[...] = source[...]

    @pl.when(pl.program_id(0) == pl.num_programs(0) - 1)
    def _():
        rows = gconv_ref.shape[0]
        gconv_ref[rows - PAD :, :] = gfix_ref[...].astype(BF16)
        pairs = conv_ref.shape[1] // LANES
        heads = bias_ref.shape[1]
        for lag in range(KERNEL):
            for n in range(pairs):
                row = lag * pairs + n
                conv_ref[lag : lag + 1, n * LANES : (n + 1) * LANES] = total_ref[row : row + 1, :]
        for n, ref in enumerate((bias_ref, rate_ref, skip_ref)):
            row = KERNEL * pairs + n
            ref[...] = total_ref[row : row + 1, 0:heads]


def local(
    queries, keys, values, attn_grad, doc_ids, conv_input, conv_weight, step_raw, step_bias,
    rate_log, skip_gain, input_coeff, output_coeff, gate_input, mix_grad,
):
    rows, width = queries.shape
    heads, channels = step_raw.shape[1], conv_input.shape[1]
    pairs = channels // LANES
    index = lax.axis_index("seq")
    groups = lax.axis_size("seq") // PLACES
    base = (index // PLACES) * PLACES * rows
    counts = jnp.sum(doc_ids[None, :] < jnp.arange(DOCS)[:, None], axis=1)
    docs = lax.dynamic_slice_in_dim(doc_ids, base, PLACES * rows)
    start = jnp.sum(jnp.where(docs[None, :] == jnp.arange(DOCS)[:, None], counts[:, None], 0), axis=0)
    where = base + jnp.arange(PLACES * rows, dtype=jnp.int32)
    low = (jnp.maximum(start, where - (WINDOW - 1)) - base + WINDOW).reshape(PLACES, rows)
    since = lax.dynamic_slice_in_dim(where - start, index % PLACES * rows, rows).astype(F32)[:, None]

    struct = jax.ShapeDtypeStruct
    vmem = pl.BlockSpec(memory_space=pltpu.VMEM)
    loose = pl.BlockSpec(memory_space=pl.ANY)
    dma = lambda n: pltpu.SemaphoreType.DMA((n,))
    head_cols = 2 * LANES
    quarter = (2, 2 * PAD, channels)
    part = quarter[1:]
    half = lambda *shape: pltpu.VMEM(shape, BF16)
    full = lambda *shape: pltpu.VMEM(shape, F32)
    flat = full(PAD, channels)
    piece = lambda n: half(n, rows, head_cols)
    red_rows = 64
    wide_shape = (rows, channels)
    mid = pl.pallas_call(
        whole_kernel,
        in_specs=[vmem] * 9 + [loose] * 7,
        out_specs=[loose] * 3 + [vmem] * 7,
        out_shape=[struct((PLACES, rows, head_cols), BF16)] * 3
        + [
            struct(wide_shape, BF16), struct(wide_shape, BF16), struct((PAD, channels), F32),
            struct((rows, heads), F32), struct((rows, LANES), F32), struct((rows, LANES), F32),
            struct((red_rows, LANES), F32),
        ],
        scratch_shapes=[
            half(rows, width), half(rows, width), half(rows, width), half(rows, width),
            half(*wide_shape), half(*wide_shape), half(*wide_shape),
            piece(PLACES), piece(PLACES), piece(PLACES), piece(PLACES),
            piece(PLACES), piece(PLACES), piece(2 * PLACES), piece(2 * PLACES),
            full(2 * PLACES, rows, head_cols), full(2 * PLACES, rows, head_cols),
            piece(PLACES), piece(PLACES), piece(PLACES), piece(PLACES),
            piece(PLACES), piece(PLACES), piece(PLACES),
            half(2 * PAD, channels), flat, full(pairs, rows, 8), full(pairs, 2, rows), full(LANES, channels),
            full(KERNEL - 1, rows, LANES), full(rows + PAD, LANES),
            full(*wide_shape), full(*wide_shape), full(*wide_shape), full(*wide_shape), full(*wide_shape),
            full(*wide_shape),
            half(PLACES, *quarter), half(PLACES, *quarter), half(*part), half(*part), full(PAD, LANES),
            half(REACH, *part), half(REACH, *part), full(REACH, PAD, LANES), full(REACH, PAD, LANES),
            half(PLACES, *quarter), half(PLACES, *quarter), full(PAD, LANES), full(PLACES, PAD, LANES),
            full(rows, rows), full(rows, rows), full(rows, rows), full(KERNEL, rows + 2 * PAD, LANES),
            full(rows, heads), full(rows, heads), full(rows, LANES // 2), full(rows, LANES // 2),
            flat, flat, flat, flat, half(rows, LANES), half(4, rows, LANES),
            full(red_rows, LANES), full(PLACES, red_rows, LANES), full(red_rows, LANES),
            full(groups, red_rows, LANES),
            dma(SENDS), dma(SENDS), dma(2 * PLACES), dma(2 * PLACES), dma(7), dma(3 * PLACES),
        ],
        name="whole",
        compiler_params=pltpu.CompilerParams(
            collective_id=0, has_side_effects=True, vmem_limit_bytes=58 * 1024 * 1024
        ),
    )(
        since, low, step_raw, step_bias[None], rate_log[None], skip_gain[None], input_coeff, output_coeff,
        conv_weight, keys, values, queries, attn_grad, conv_input, gate_input, mix_grad,
    )
    steps = 4
    tall = lambda cols: pl.BlockSpec((rows // steps, cols), lambda n: (n, 0))
    piled = pl.BlockSpec((PLACES, rows // steps, head_cols), lambda n: (0, n, 0))
    whole = lambda *shape: pl.BlockSpec(shape, lambda n: (0, 0))
    *outs, conv, bias, rate, skip = pl.pallas_call(
        finish_kernel,
        grid=(steps,),
        in_specs=[piled] * 3
        + [
            tall(channels), tall(channels), whole(PAD, channels), tall(heads), tall(LANES), tall(LANES),
            whole(red_rows, LANES),
        ],
        out_specs=[tall(width)] * 3
        + [tall(channels), tall(channels), tall(heads), tall(LANES), tall(LANES), whole(KERNEL, channels)]
        + [whole(1, heads)] * 3,
        out_shape=[struct((rows, width), BF16)] * 3
        + [
            struct(wide_shape, BF16), struct(wide_shape, BF16), struct((rows, heads), F32),
            struct((rows, LANES), F32), struct((rows, LANES), F32), struct((KERNEL, channels), F32),
        ]
        + [struct((1, heads), F32)] * 3,
        name="finish",
        compiler_params=pltpu.CompilerParams(dimension_semantics=("arbitrary",)),
    )(*mid)
    return (*outs, conv, bias[0], rate[0], skip[0])


def solution(mesh):
    sharded = P("seq", "head")
    return jax.shard_map(
        local,
        mesh=mesh,
        in_specs=(
            sharded, sharded, sharded, sharded, P(), sharded, P(None, "head"), sharded,
            P("head"), P("head"), P("head"), P("seq", None), P("seq", None), sharded, sharded,
        ),
        out_specs=(
            sharded, sharded, sharded, sharded, sharded, sharded,
            P("seq", None), P("seq", None), P(None, "head"), P("head"), P("head"), P("head"),
        ),
        check_vma=False,
    )
```

time: 118 us -> 97.9 us (0.83)
  local copies, waits for them, and re-layouts: 15.2 us -> 4.59 us
  Pallas kernels: 100 us -> 91.3 us
    pallas_call x1 -> x2, Pallas kernels: 100 us -> 91.3 us  [the longest x1 86.3 us: local(): pl.pallas_call(whole_kernel, in_specs=[vmem] * 9 + [loose] * 7, out_specs...]
    unnamed x29 -> x6, local copies, waits for them, and re-layouts: 10.7 us -> 3.1 us
    slice x1 -> x0, local copies, waits for them, and re-layouts: 1.43 us -> none  [local(): total[:KERNEL]]
    squeeze x1 -> x0, local copies, waits for them, and re-layouts: 1.31 us -> none  [local(): total[6, :heads]]
where the time goes in v2:
time: 97.9 us; the launch traced here: 97.5 us
  Pallas kernels  91.3 us (93%)
  local copies, waits for them, and re-layouts  4.59 us (5%)
    pallas_call x1, Pallas kernels, local(): pl.pallas_call(whole_kernel, in_specs=[vmem] * 9 + [loose] * 7, out_specs...  86.3 us
    pallas_call x1, Pallas kernels, local(): pl.pallas_call(finish_kernel, grid=(steps,), in_specs=[piled] * 3 + [tall...  4.92 us
    unnamed x6, local copies, waits for them, and re-layouts  3.1 us

profile of v2, /device:TPU:0, one launch (start us, length us, event | category | flops | bytes accessed | tf_op | source)
XLA Modules:
  0.0 97.5 jit_solution(11340351316667830148)
XLA Ops:
  0.6 0.0 copy-start
  0.7 0.7 copy-done
  1.4 0.2 convert_reduce_fusion
  1.6 0.0 dynamic-slice-start
  1.6 0.7 dynamic-slice-done
  2.3 0.1 select_reduce_fusion
  2.4 0.1 dynamic-slice_convert_fusion
  2.5 0.6 subtract_add_fusion.low_ref
  3.1 0.0 copy-start.1
  3.1 0.8 copy.32.since_ref
  3.9 0.0 copy-done.1
  3.9 0.8 copy.33.step_ref
  4.6 86.3 %whole.1 = (bf16[4,256,256]{2,1,0:T(8,128)(2,1)}, bf16[4,256,256]{2,1,0:T(8,128)(2,1)}, bf16[4,256,256]{2,1,0:T(8,128)(2,1)}, bf16[256,1792]{1,0:T(8,128)(2,1)},...) custom-call(f32[256,1]{1,0:T(8,128)} %copy.32.since_ref, ...), custom_call_target="tpu_custom_call" | custom-call | tf_op jit(solution)/shard_map/whole/pallas_call | solution.py:546
  91.0 4.9 %finish.1 = (bf16[256,896]{1,0:T(8,128)(2,1)}, bf16[256,896]{1,0:T(8,128)(2,1)}, bf16[256,896]{1,0:T(8,128)(2,1)}, bf16[256,1792]{1,0:T(8,128)(2,1)}, bf16[256,1...) custom-call(bf16[4,256,256]{2,1,0:T(8,128)(2,1)} %get-tuple-element., ...), custom_call_target="tpu_custom_call" | custom-call | tf_op jit(solution)/shard_map/finish/pallas_call | solution.py:590
  95.9 1.6 %copy.34 = f32[256,28]{0,1:T(8,128)} copy(f32[256,28]{1,0:T(8,128)} %get-tuple-element.85) | data formatting | bytes 57344
  (2 shorter events, 0.0 us)
Async XLA Ops:
  0.6 0.8 copy-start
  1.6 0.7 dynamic-slice-start
  3.1 0.8 copy-start.1

commit v3 on v2

--- a/solution.py
+++ b/solution.py
@@ -77,9 +77,9 @@
     return jnp.where(lower, cols[:, 2 * index : 2 * index + 1], cols[:, 2 * index + 1 : 2 * index + 2])
 
 
-def fill_masks(since_ref, mask_ref):
+def fill_masks(since, mask_ref):
     for lag in range(1, KERNEL):
-        mask_ref[lag - 1] = jnp.broadcast_to((since_ref[...] >= lag).astype(F32), mask_ref.shape[1:])
+        mask_ref[lag - 1] = jnp.broadcast_to((since >= lag).astype(F32), mask_ref.shape[1:])
 
 
 def conv_pre(conv, tail, wt, mask_ref, xp_ref):
@@ -100,10 +100,10 @@
 
 
 def whole_kernel(
-    since_ref, low_ref, step_ref, bias_ref, rate_ref, skip_ref, b_ref, c_ref, weight_ref,
+    small_hbm,
     k_hbm, v_hbm, q_hbm, do_hbm, conv_hbm, gate_hbm, mix_hbm,
-    dq_in, dk_in, dv_in, gconv_ref, ggate_ref, gfix_ref, gstep_ref, gin_ref, gout_ref, total_ref,
-    k_ref, v_ref, q_ref, do_ref, conv_ref, gate_ref, mix_ref,
+    dq_in, dk_in, dv_in, gconv_hbm, ggate_hbm, gfix_ref, gstep_ref, gin_ref, gout_ref, total_ref,
+    small_refs, gconv_ref, ggate_ref, low_ref, since_ref, turn_ref, turn_back, k_ref, v_ref, q_ref, do_ref, conv_ref, gate_ref, mix_ref,
     k_pack, v_pack, q_pack, do_pack, q_all, do_all, k_all, v_all, dk_all, dv_all,
     dk_out, dv_out, dk_back, dv_back, dq_own, dk_own, dv_own,
     tail_buf, wt_ref, cols_ref, rowc_ref, spread_ref, mask_ref, xp_ref,
@@ -111,11 +111,12 @@
     ends_ref, a_ref, end_out, cot_out, g_out, e_in, c_in, ge_in, gc_in, chain_out, state_ref, t_out, t_all,
     mix_bias, pair_ref, dpair_ref, dpad_ref, z_ref, u_ref, db_ref, dc_ref,
     sums_ref, edge_ref, end_ref, spill_ref, coef_out, coef_all, red_out, red_a, red_mid, red_b,
-    sends, receives, back_sends, back_receives, loads, keeps,
+    sends, receives, back_sends, back_receives, loads, keeps, writes, small_loads,
 ):
     group, place, groups = where_am_i()
     head, head_count = lax.axis_index("head"), lax.axis_size("head")
-    rows, heads = step_ref.shape
+    doc_ref, step_ref, bias_ref, rate_ref, skip_ref, b_ref, c_ref, weight_ref = small_refs
+    heads, rows = step_ref.shape
     channels = conv_ref.shape[1]
     pairs = channels // LANES
     peers = [lax.rem(place + d, PLACES) for d in range(1, PLACES)]
@@ -127,6 +128,12 @@
     )):
         fetches.append(pltpu.make_async_copy(source, target, loads.at[n]))
         fetches[-1].start()
+    small_fetches = [
+        pltpu.make_async_copy(source, target, small_loads.at[n])
+        for n, (source, target) in enumerate(zip(small_hbm, small_refs))
+    ]
+    for fetch in small_fetches:
+        fetch.start()
     partners = [shard(group + far, place, groups) for far in range(1, groups)]
     partners += [shard(group, peer, groups) for peer in peers]
     last, first = place == PLACES - 1, place == 0
@@ -162,10 +169,33 @@
     pack(q_ref, q_pack)
     fetches[4].wait()
     pack(do_ref, do_pack)
-    near = spread(q_pack, q_all, 0) + spread(do_pack, do_all, 0)
-
-    since = since_ref[...]
-    raw = step_ref[...] + bias_ref[...]
+
+    for fetch in small_fetches:
+        fetch.wait()
+    per_row = rows // LANES
+    docs = doc_ref[pl.ds(pl.multiple_of(group * PLACES * per_row, PLACES * per_row), PLACES * per_row), :]
+    everyone_doc = doc_ref[...]
+    begin = jnp.zeros(docs.shape, F32)
+    for doc in range(1, DOCS):
+        count = jnp.sum((everyone_doc < doc).astype(F32), axis=0, keepdims=True)
+        count = jnp.sum(count, axis=1, keepdims=True)
+        begin = jnp.where(docs == doc, count, begin)
+    where = (
+        lax.broadcasted_iota(jnp.int32, docs.shape, 0) * LANES
+        + lax.broadcasted_iota(jnp.int32, docs.shape, 1)
+        + group * (PLACES * rows)
+    ).astype(F32)
+    low = jnp.maximum(begin, where - (WINDOW - 1)) - (group * (PLACES * rows) - WINDOW).astype(F32)
+    since_ref[...] = where - begin
+    for n in range(PLACES * per_row):
+        b, side = n // per_row, n % per_row
+        low_ref[b : b + 1, side * LANES : (side + 1) * LANES] = low[n : n + 1]
+    row = jnp.concatenate([since_ref[pl.ds(place * per_row + n, 1), :] for n in range(per_row)], axis=1)
+    since = jnp.broadcast_to(row, (PAD, rows)).T[:, 0:1]
+
+    turn_ref[...] = jnp.zeros_like(turn_ref)
+    turn_ref[0:heads, :] = step_ref[...]
+    raw = turn_ref[...].T[:, 0:heads] + bias_ref[...]
     step = jnp.maximum(raw, 0.0) + jnp.log1p(jnp.exp(-jnp.abs(raw)))
     rate = jnp.exp(rate_ref[...])
     log_decay = -step * rate
@@ -189,7 +219,7 @@
     spread_ref[...] = spreader(heads, channels)
     wt_ref[0:KERNEL, :] = weight_ref[...]
     wt_ref[KERNEL : KERNEL + 1, :] = dot(skip_ref[...], spread_ref[0:heads, :], 1, 0, EXACT)
-    fill_masks(since_ref, mask_ref)
+    fill_masks(since, mask_ref)
     lower = lax.broadcasted_iota(jnp.int32, (rows, LANES), 1) < LANES // 2
     b_part, c_part = group_part(b_ref), group_part(c_ref)
     fetches[5].wait()
@@ -226,14 +256,14 @@
             source = lax.rem(place + PLACES - d, PLACES)
             far.append(post.send(target.at[PLACES + source], target.at[source], ahead))
 
-    lax.fori_loop(0, pairs // 4, ends, 0)
+    lax.fori_loop(0, 2 * pairs // 3, ends, 0)
     pass_on(near_k, k_all)
-    lax.fori_loop(pairs // 4, 3 * pairs // 4, ends, 0)
+    lax.fori_loop(2 * pairs // 3, pairs, ends, 0)
+
+    a_copies = [post.send(ends_ref.at[peer], a_ref.at[place], shard(group, peer, groups)) for peer in peers]
+    near = spread(q_pack, q_all, 0) + spread(do_pack, do_all, 0)
+    a_ref[place] = ends_ref[place]
     pass_on(near_v, v_all)
-    lax.fori_loop(3 * pairs // 4, pairs, ends, 0)
-
-    a_copies = [post.send(ends_ref.at[peer], a_ref.at[place], shard(group, peer, groups)) for peer in peers]
-    a_ref[place] = ends_ref[place]
     for mine, everyone, offset in (
         (k_pack, k_all, PLACES), (v_pack, v_all, PLACES), (q_pack, q_all, 0), (do_pack, do_all, 0)
     ):
@@ -289,28 +319,9 @@
         b_copies.append(post.send(end_out, e_in.at[away - 1], later))
         b_copies.append(post.send(cot_out, c_in.at[away - 1], earlier))
     lax.fori_loop(pairs // 3, pairs, within, 0)
-    for copy in b_copies:
-        copy.wait()
-    before = dot(ge_in[...].reshape(REACH * PAD, LANES), spread_ref[...], 1, 0, EXACT)
-    after = dot(gc_in[...].reshape(REACH * PAD, LANES), spread_ref[...], 1, 0, EXACT)
-    state = e_in[REACH - 1].astype(F32)
-    cot = c_in[REACH - 1].astype(F32) * (group + REACH < groups).astype(F32)
-    for away in range(REACH - 2, -1, -1):
-        state = e_in[away].astype(F32) + before[PAD * away : PAD * away + 1] * state
-        cot = (c_in[away].astype(F32) + after[PAD * away : PAD * away + 1] * cot) * (
-            group + away + 1 < groups
-        ).astype(F32)
-    for n in range(PLACES):
-        chain_out[n, 0] = state.astype(BF16)
-        state = end_of(n) + decay[n] * state
-        m = PLACES - 1 - n
-        chain_out[m, 1] = cot.astype(BF16)
-        cot = cot_of(m) + decay[m] * cot
-    state_copies = [
-        post.send(chain_out.at[peer], state_ref.at[place], shard(group, peer, groups)) for peer in peers
-    ]
-    state_ref[place] = chain_out[place]
-
+    dpair = dpair_ref[...]
+    dc_ref[...] = dot(dpair, b_part.astype(F32), 1, 0, EXACT)
+    db_ref[...] = dot(dpair, c_part.astype(F32), 0, 0, EXACT)
     for copy in near + far:
         copy.wait()
 
@@ -319,6 +330,8 @@
             src_ref=source.at[b], dst_ref=target.at[b], send_sem=back_sends.at[n],
             recv_sem=back_receives.at[n], device_id=behind, device_id_type=pl.DeviceIdType.MESH,
         )
+
+    below = i.astype(F32)
 
     def block(b, carry):
         q = q_all[b]
@@ -328,7 +341,7 @@
         scores = []
         top = None
         for gap in range(PLACES + 1):
-            allowed = i + at[gap] * rows >= low
+            allowed = below >= low - jnp.asarray(at[gap] * rows).astype(F32)
             if gap == 0:
                 allowed = allowed & (j >= i)
             s = jnp.where(allowed, dot(k_all[at[gap]], q, 1, 1) * SCALE, NEG_FILL)
@@ -364,7 +377,30 @@
         back_copy(dk_out, dk_back, b, b).start()
         return carry
 
-    lax.fori_loop(0, PLACES, block, 0)
+    lax.fori_loop(0, PLACES // 2, block, 0)
+    for copy in b_copies:
+        copy.wait()
+    before = dot(ge_in[...].reshape(REACH * PAD, LANES), spread_ref[...], 1, 0, EXACT)
+    after = dot(gc_in[...].reshape(REACH * PAD, LANES), spread_ref[...], 1, 0, EXACT)
+    state = e_in[REACH - 1].astype(F32)
+    cot = c_in[REACH - 1].astype(F32) * (group + REACH < groups).astype(F32)
+    for away in range(REACH - 2, -1, -1):
+        state = e_in[away].astype(F32) + before[PAD * away : PAD * away + 1] * state
+        cot = (c_in[away].astype(F32) + after[PAD * away : PAD * away + 1] * cot) * (
+            group + away + 1 < groups
+        ).astype(F32)
+    for n in range(PLACES):
+        chain_out[n, 0] = state.astype(BF16)
+        state = end_of(n) + decay[n] * state
+        m = PLACES - 1 - n
+        chain_out[m, 1] = cot.astype(BF16)
+        cot = cot_of(m) + decay[m] * cot
+    state_copies = [
+        post.send(chain_out.at[peer], state_ref.at[place], shard(group, peer, groups)) for peer in peers
+    ]
+    state_ref[place] = chain_out[place]
+
+    lax.fori_loop(PLACES // 2, PLACES, block, 0)
     for b in range(PLACES):
         back_copy(dv_out, dv_back, b, PLACES + b).start()
     kept = []
@@ -435,10 +471,14 @@
     lane = lax.broadcasted_iota(jnp.int32, (rows, heads), 1)
     for copy in state_copies:
         copy.wait()
-    lax.fori_loop(0, pairs // 2, across, 0)
+    lax.fori_loop(0, 2 * pairs // 3, across, 0)
     whole_sum(dk_out, dk_back, dk_all, dk_own, 0, SCALE)
     give_back(dk_own, dk_in)
-    lax.fori_loop(pairs // 2, pairs, across, 0)
+    lax.fori_loop(2 * pairs // 3, pairs, across, 0)
+    written = []
+    for n, (source, target) in enumerate(((gconv_ref, gconv_hbm), (ggate_ref, ggate_hbm))):
+        written.append(pltpu.make_async_copy(source, target, writes.at[n]))
+        written[-1].start()
 
     spill_copy = post.send(edge_ref, spill_ref, former)
     per_head = dot(sums_ref[...], spread_ref[...], 1, 1, EXACT)[:, 0:heads]
@@ -446,19 +486,20 @@
     dcum = z_ref[...] + jnp.where(t == rows - 1, last_row, 0.0)
     dlog = dot(tri, dcum, 0, 0, EXACT)
     grad_step = (u_ref[...] - dlog * rate) * jax.nn.sigmoid(raw)
-    gstep_ref[...] = grad_step
+    turn_back[...] = jnp.zeros_like(turn_back)
+    turn_back[:, 0:heads] = grad_step
+    gstep_ref[...] = turn_back[...].T[0:heads, :]
     small = KERNEL * pairs
     red_out[small : small + 1, 0:heads] = jnp.sum(grad_step, axis=0, keepdims=True)
     red_out[small + 1 : small + 2, 0:heads] = jnp.sum(dlog * log_decay, axis=0, keepdims=True)
     red_out[small + 2 : small + 3, 0:heads] = per_head[0:1]
     reds = [post.send(red_out, red_a.at[place], shard(group, peer, groups)) for peer in peers]
     red_a[place] = red_out[...]
-    dpair = dpair_ref[...]
-    dc_ref[...] += dot(dpair, b_part.astype(F32), 1, 0, EXACT)
-    db_ref[...] += dot(dpair, c_part.astype(F32), 0, 0, EXACT)
     coef_out[...] = jnp.concatenate([db_ref[...], dc_ref[...]], axis=1).astype(BF16)
     coefs = [post.send(coef_out, coef_all.at[head], peer) for peer in head_peers]
     coef_all[head] = coef_out[...]
+    whole_sum(dv_out, dv_back, dv_all, dv_own, PLACES, 1.0)
+    give_back(dv_own, dv_in)
     for copy in reds:
         copy.wait()
     red_mid[...] = red_a[0] + red_a[1] + red_a[2] + red_a[3]
@@ -466,8 +507,6 @@
         post.send(red_mid, red_b.at[group], shard(group + away, place, groups)) for away in range(1, groups)
     ]
     red_b[group] = red_mid[...]
-    whole_sum(dv_out, dv_back, dv_all, dv_own, PLACES, 1.0)
-    give_back(dv_own, dv_in)
     spill_copy.wait()
     gfix_ref[...] = end_ref[...] + spill_ref[...]
     for copy in coefs:
@@ -482,7 +521,7 @@
     for n in range(1, groups):
         total = total + red_b[n]
     total_ref[...] = total
-    for copy in kept:
+    for copy in kept + written:
         copy.wait()
 
 
@@ -520,16 +559,7 @@
     rows, width = queries.shape
     heads, channels = step_raw.shape[1], conv_input.shape[1]
     pairs = channels // LANES
-    index = lax.axis_index("seq")
     groups = lax.axis_size("seq") // PLACES
-    base = (index // PLACES) * PLACES * rows
-    counts = jnp.sum(doc_ids[None, :] < jnp.arange(DOCS)[:, None], axis=1)
-    docs = lax.dynamic_slice_in_dim(doc_ids, base, PLACES * rows)
-    start = jnp.sum(jnp.where(docs[None, :] == jnp.arange(DOCS)[:, None], counts[:, None], 0), axis=0)
-    where = base + jnp.arange(PLACES * rows, dtype=jnp.int32)
-    low = (jnp.maximum(start, where - (WINDOW - 1)) - base + WINDOW).reshape(PLACES, rows)
-    since = lax.dynamic_slice_in_dim(where - start, index % PLACES * rows, rows).astype(F32)[:, None]
-
     struct = jax.ShapeDtypeStruct
     vmem = pl.BlockSpec(memory_space=pltpu.VMEM)
     loose = pl.BlockSpec(memory_space=pl.ANY)
@@ -543,17 +573,23 @@
     piece = lambda n: half(n, rows, head_cols)
     red_rows = 64
     wide_shape = (rows, channels)
+    small = [
+        doc_ids.reshape(-1, LANES), step_raw.T, step_bias[None], rate_log[None], skip_gain[None],
+        input_coeff, output_coeff, conv_weight,
+    ]
     mid = pl.pallas_call(
         whole_kernel,
-        in_specs=[vmem] * 9 + [loose] * 7,
-        out_specs=[loose] * 3 + [vmem] * 7,
+        in_specs=[[loose] * 8] + [loose] * 7,
+        out_specs=[loose] * 5 + [vmem] * 5,
         out_shape=[struct((PLACES, rows, head_cols), BF16)] * 3
         + [
             struct(wide_shape, BF16), struct(wide_shape, BF16), struct((PAD, channels), F32),
-            struct((rows, heads), F32), struct((rows, LANES), F32), struct((rows, LANES), F32),
+            struct((heads, rows), F32), struct((rows, LANES), F32), struct((rows, LANES), F32),
             struct((red_rows, LANES), F32),
         ],
         scratch_shapes=[
+            [pltpu.VMEM(a.shape, a.dtype) for a in small], half(*wide_shape), half(*wide_shape),
+            full(PAD, rows), full(PLACES * rows // LANES, LANES), full(LANES, rows), full(rows, LANES),
             half(rows, width), half(rows, width), half(rows, width), half(rows, width),
             half(*wide_shape), half(*wide_shape), half(*wide_shape),
             piece(PLACES), piece(PLACES), piece(PLACES), piece(PLACES),
@@ -573,15 +609,14 @@
             flat, flat, flat, flat, half(rows, LANES), half(4, rows, LANES),
             full(red_rows, LANES), full(PLACES, red_rows, LANES), full(red_rows, LANES),
             full(groups, red_rows, LANES),
-            dma(SENDS), dma(SENDS), dma(2 * PLACES), dma(2 * PLACES), dma(7), dma(3 * PLACES),
+            dma(SENDS), dma(SENDS), dma(2 * PLACES), dma(2 * PLACES), dma(7), dma(3 * PLACES), dma(2), dma(8),
         ],
         name="whole",
         compiler_params=pltpu.CompilerParams(
             collective_id=0, has_side_effects=True, vmem_limit_bytes=58 * 1024 * 1024
         ),
     )(
-        since, low, step_raw, step_bias[None], rate_log[None], skip_gain[None], input_coeff, output_coeff,
-        conv_weight, keys, values, queries, attn_grad, conv_input, gate_input, mix_grad,
+        small, keys, values, queries, attn_grad, conv_input, gate_input, mix_grad,
     )
     steps = 4
     tall = lambda cols: pl.BlockSpec((rows // steps, cols), lambda n: (n, 0))
@@ -592,21 +627,22 @@
         grid=(steps,),
         in_specs=[piled] * 3
         + [
-            tall(channels), tall(channels), whole(PAD, channels), tall(heads), tall(LANES), tall(LANES),
+            tall(channels), tall(channels), whole(PAD, channels), whole(heads, rows), tall(LANES), tall(LANES),
             whole(red_rows, LANES),
         ],
         out_specs=[tall(width)] * 3
-        + [tall(channels), tall(channels), tall(heads), tall(LANES), tall(LANES), whole(KERNEL, channels)]
+        + [tall(channels), tall(channels), whole(heads, rows), tall(LANES), tall(LANES), whole(KERNEL, channels)]
         + [whole(1, heads)] * 3,
         out_shape=[struct((rows, width), BF16)] * 3
         + [
-            struct(wide_shape, BF16), struct(wide_shape, BF16), struct((rows, heads), F32),
+            struct(wide_shape, BF16), struct(wide_shape, BF16), struct((heads, rows), F32),
             struct((rows, LANES), F32), struct((rows, LANES), F32), struct((KERNEL, channels), F32),
         ]
         + [struct((1, heads), F32)] * 3,
         name="finish",
         compiler_params=pltpu.CompilerParams(dimension_semantics=("arbitrary",)),
     )(*mid)
+    outs[5] = outs[5].T
     return (*outs, conv, bias[0], rate[0], skip[0])
 
 

time: 97.9 us -> 82.1 us (0.84)
  Pallas kernels: 91.3 us -> 80.5 us
  local copies, waits for them, and re-layouts: 4.59 us -> 0 us
    pallas_call x1, Pallas kernels: 86.3 us -> 75.6 us  [local(): pl.pallas_call(whole_kernel, in_specs=[[loose] * 8] + [loose] * 7, out_sp...]
    unnamed x6 -> x0, local copies, waits for them, and re-layouts: 3.1 us -> none
where the time goes in v3:
time: 82.1 us; the launch traced here: 81.3 us
  Pallas kernels  80.5 us (98%)
    pallas_call x1, Pallas kernels, local(): pl.pallas_call(whole_kernel, in_specs=[[loose] * 8] + [loose] * 7, out_sp...  75.6 us
    pallas_call x1, Pallas kernels, local(): pl.pallas_call(finish_kernel, grid=(steps,), in_specs=[piled] * 3 + [tall...  4.88 us

profile of v3, /device:TPU:0, one launch (start us, length us, event | category | flops | bytes accessed | tf_op | source)
XLA Modules:
  0.0 81.3 jit_solution(17219351090749638945)
XLA Ops:
  0.7 75.6 %whole.1 = (bf16[4,256,256]{2,1,0:T(8,128)(2,1)}, bf16[4,256,256]{2,1,0:T(8,128)(2,1)}, bf16[4,256,256]{2,1,0:T(8,128)(2,1)}, bf16[256,1792]{1,0:T(8,128)(2,1)},...) custom-call(s32[64,128]{1,0:T(8,128)} %bitcast.9, ...), custom_call_target="tpu_custom_call" | custom-call | tf_op jit(solution)/shard_map/whole/pallas_call | solution.py:580
  76.3 4.9 %finish.1 = (bf16[256,896]{1,0:T(8,128)(2,1)}, bf16[256,896]{1,0:T(8,128)(2,1)}, bf16[256,896]{1,0:T(8,128)(2,1)}, bf16[256,1792]{1,0:T(8,128)(2,1)}, bf16[256,1...) custom-call(bf16[4,256,256]{2,1,0:T(8,128)(2,1)} %get-tuple-element., ...), custom_call_target="tpu_custom_call" | custom-call | tf_op jit(solution)/shard_map/finish/pallas_call | solution.py:625

commit v4 on v3

--- a/solution.py
+++ b/solution.py
@@ -18,7 +18,7 @@
 F32 = jnp.float32
 BF16 = jnp.bfloat16
 NEG_FILL = -1e30
-SENDS = 69
+SENDS = 79
 SCALE = HEAD_DIM ** (-0.5)
 
 
@@ -99,12 +99,37 @@
     return jnp.where(first, whole[:, :half], whole[:, half:]).astype(BF16)
 
 
+def fold(value, target, at=()):
+    rows, (keep, quarter) = value.shape[0], (3 * value.shape[0] // 4, value.shape[0] // 4)
+    target[(*at, slice(0, rows), slice(None))] = value[:, 0:LANES]
+    rest, width = HEAD_DIM - LANES, LANES // 4
+    target[(*at, slice(rows, rows + keep), slice(0, rest))] = value[0:keep, LANES:HEAD_DIM]
+    for n in range(3):
+        target[(*at, slice(rows + n * quarter, rows + (n + 1) * quarter), slice(rest, LANES))] = value[
+            keep:, LANES + n * width : LANES + (n + 1) * width
+        ]
+
+
+def unfold(source, source_at, target, target_at, offset=0):
+    rows = 4 * source.shape[-2] // 7
+    keep, quarter, rest, width = 3 * rows // 4, rows // 4, HEAD_DIM - LANES, LANES // 4
+    put = lambda a, b, c, d, value: target.__setitem__((*target_at, slice(a, b), slice(offset + c, offset + d)), value)
+    get = lambda a, b, c, d: source[(*source_at, slice(a, b), slice(c, d))]
+    put(0, rows, 0, LANES, get(0, rows, 0, LANES))
+    put(0, keep, LANES, HEAD_DIM, get(rows, rows + keep, 0, rest))
+    for n in range(3):
+        put(
+            keep, rows, LANES + n * width, LANES + (n + 1) * width,
+            get(rows + n * quarter, rows + (n + 1) * quarter, rest, LANES),
+        )
+
+
 def whole_kernel(
     small_hbm,
     k_hbm, v_hbm, q_hbm, do_hbm, conv_hbm, gate_hbm, mix_hbm,
-    dq_in, dk_in, dv_in, gconv_hbm, ggate_hbm, gfix_ref, gstep_ref, gin_ref, gout_ref, total_ref,
-    small_refs, gconv_ref, ggate_ref, low_ref, since_ref, turn_ref, turn_back, k_ref, v_ref, q_ref, do_ref, conv_ref, gate_ref, mix_ref,
-    k_pack, v_pack, q_pack, do_pack, q_all, do_all, k_all, v_all, dk_all, dv_all,
+    dq_in, dk_in, dv_in, gconv_hbm, ggate_hbm, gfix_hbm, gstep_hbm, gin_hbm, gout_hbm, total_ref,
+    small_refs, gfix_ref, gstep_ref, gin_ref, gout_ref, gconv_ref, ggate_ref, low_ref, since_ref, turn_ref, turn_back, k_ref, v_ref, q_ref, do_ref, conv_ref, gate_ref, mix_ref,
+    k_pack, v_pack, q_pack, do_pack, q_in, do_in, k_in, v_in, own_fold, q_all, do_all, k_all, v_all, dk_all, dv_all,
     dk_out, dv_out, dk_back, dv_back, dq_own, dk_own, dv_own,
     tail_buf, wt_ref, cols_ref, rowc_ref, spread_ref, mask_ref, xp_ref,
     act_all, slope_all, dy_all, cg_all, inner_all, dx_all,
@@ -146,8 +171,7 @@
 
     def pack(source, target):
         for r in range(PLACES):
-            target[r, :, 0:HEAD_DIM] = source[:, r * HEAD_DIM : (r + 1) * HEAD_DIM]
-            target[r, :, HEAD_DIM:] = jnp.zeros((rows, target.shape[2] - HEAD_DIM), BF16)
+            fold(source[:, r * HEAD_DIM : (r + 1) * HEAD_DIM], target, (r,))
 
     def spread(source, target, offset):
         return [
@@ -156,15 +180,15 @@
 
     fetches[0].wait()
     pack(k_ref, k_pack)
-    fetches[1].wait()
-    pack(v_ref, v_pack)
     fetches[2].wait()
     wait_partners()
     tail_copy = post.send(conv_ref.at[rows - 2 * PAD :, :], tail_buf, follower)
-    far = [post.send(k_pack.at[place], k_all.at[place], ahead)]
-    near_k = spread(k_pack, k_all, PLACES)
-    far.append(post.send(v_pack.at[place], v_all.at[place], ahead))
-    near_v = spread(v_pack, v_all, PLACES)
+    far = [post.send(k_pack.at[place], k_in.at[place], ahead)]
+    near_k = spread(k_pack, k_in, PLACES)
+    fetches[1].wait()
+    pack(v_ref, v_pack)
+    far.append(post.send(v_pack.at[place], v_in.at[place], ahead))
+    near_v = spread(v_pack, v_in, PLACES)
     fetches[3].wait()
     pack(q_ref, q_pack)
     fetches[4].wait()
@@ -257,17 +281,29 @@
             far.append(post.send(target.at[PLACES + source], target.at[source], ahead))
 
     lax.fori_loop(0, 2 * pairs // 3, ends, 0)
-    pass_on(near_k, k_all)
+    pass_on(near_k, k_in)
     lax.fori_loop(2 * pairs // 3, pairs, ends, 0)
 
     a_copies = [post.send(ends_ref.at[peer], a_ref.at[place], shard(group, peer, groups)) for peer in peers]
-    near = spread(q_pack, q_all, 0) + spread(do_pack, do_all, 0)
+    near = spread(q_pack, q_in, 0) + spread(do_pack, do_in, 0)
     a_ref[place] = ends_ref[place]
-    pass_on(near_v, v_all)
+    pass_on(near_v, v_in)
     for mine, everyone, offset in (
-        (k_pack, k_all, PLACES), (v_pack, v_all, PLACES), (q_pack, q_all, 0), (do_pack, do_all, 0)
+        (k_pack, k_in, PLACES), (v_pack, v_in, PLACES), (q_pack, q_in, 0), (do_pack, do_in, 0)
     ):
         everyone[offset + place] = mine[place]
+
+    def open_up(pairs_of, first, count):
+        def one(n, carry):
+            for source, target in pairs_of:
+                unfold(source, (n,), target, (n,))
+            return carry
+
+        lax.fori_loop(first, first + count, one, 0)
+
+    for ref in (k_all, v_all, q_all, do_all):
+        ref[:, :, LANES:] = jnp.zeros((ref.shape[0], rows, LANES), BF16)
+    open_up(((k_in, k_all), (v_in, v_all)), PLACES, PLACES)
     dk_all[...] = jnp.zeros_like(dk_all)
     dv_all[...] = jnp.zeros_like(dv_all)
 
@@ -322,8 +358,12 @@
     dpair = dpair_ref[...]
     dc_ref[...] = dot(dpair, b_part.astype(F32), 1, 0, EXACT)
     db_ref[...] = dot(dpair, c_part.astype(F32), 0, 0, EXACT)
-    for copy in near + far:
-        copy.wait()
+    for copy in near:
+        copy.wait()
+    open_up(((q_in, q_all), (do_in, do_all)), 0, PLACES)
+    for copy in far:
+        copy.wait()
+    open_up(((k_in, k_all), (v_in, v_all)), 0, PLACES)
 
     def back_copy(source, target, b, n):
         return pltpu.make_async_remote_copy(
@@ -371,10 +411,10 @@
             dk_all[at[gap]] += dot(ds, q, 1, 0)
             part = dot(ds, k_all[at[gap]], 0, 0)
             dq = part if dq is None else dq + part
-        dq_own[b] = (dq * SCALE).astype(BF16)
-        dk_out[b] = dk_all[b].astype(BF16)
-        dv_out[b] = dv_all[b].astype(BF16)
+        fold((dq * SCALE).astype(BF16), dq_own, (b,))
+        fold(dk_all[b].astype(BF16), dk_out, (b,))
         back_copy(dk_out, dk_back, b, b).start()
+        fold(dv_all[b].astype(BF16), dv_out, (b,))
         return carry
 
     lax.fori_loop(0, PLACES // 2, block, 0)
@@ -444,12 +484,12 @@
         dc_ref[...] += dot((enter * dy).astype(BF16), state, 1, 1)
         db_ref[...] += dot((to_end * x_wide).astype(BF16), end_cot, 1, 1)
         dpre = (dx * size + skip * dy) * slope_all[:, lanes]
-        red_out[pl.ds(n, 1), :] = jnp.sum(dpre * xp_ref[PAD:, :], axis=0, keepdims=True)
+        red_out[pl.ds(KERNEL * n, 1), :] = jnp.sum(dpre * xp_ref[PAD:, :], axis=0, keepdims=True)
         dpad_ref[0, PAD : PAD + rows, :] = dpre
         grown = wt[0:1, :] * dpad_ref[0, 0 : rows + PAD, :]
         for lag in range(1, KERNEL):
             masked = dpre * mask_ref[lag - 1]
-            red_out[pl.ds(lag * pairs + n, 1), :] = jnp.sum(
+            red_out[pl.ds(KERNEL * n + lag, 1), :] = jnp.sum(
                 masked * xp_ref[PAD - lag : PAD - lag + rows, :], axis=0, keepdims=True
             )
             dpad_ref[lag, PAD : PAD + rows, :] = masked
@@ -465,20 +505,44 @@
 
     def whole_sum(source, target, total, out, offset, factor):
         for b in range(PLACES):
+            fold(total[PLACES + b], own_fold)
             back_copy(source, target, b, offset + b).wait()
-            out[b] = ((total[PLACES + b] + target[b].astype(F32)) * factor).astype(BF16)
+            out[b] = ((own_fold[...] + target[b].astype(F32)) * factor).astype(BF16)
 
     lane = lax.broadcasted_iota(jnp.int32, (rows, heads), 1)
     for copy in state_copies:
         copy.wait()
-    lax.fori_loop(0, 2 * pairs // 3, across, 0)
+    def exchange(part):
+        return [
+            post.send(red_out.at[part], red_a.at[place, part], shard(group, peer, groups)) for peer in peers
+        ]
+
+    def widen(part, copies):
+        red_a[place, part] = red_out[part]
+        for copy in copies:
+            copy.wait()
+        red_mid[part] = red_a[0, part] + red_a[1, part] + red_a[2, part] + red_a[3, part]
+        red_b[group, part] = red_mid[part]
+        return [
+            post.send(red_mid.at[part], red_b.at[group, part], shard(group + away, place, groups))
+            for away in range(1, groups)
+        ]
+
+    upper, under = pl.ds(0, 4 * PAD), pl.ds(4 * PAD, 4 * PAD)
+    lax.fori_loop(0, 4 * PAD // KERNEL, across, 0)
+    early = exchange(upper)
     whole_sum(dk_out, dk_back, dk_all, dk_own, 0, SCALE)
     give_back(dk_own, dk_in)
-    lax.fori_loop(2 * pairs // 3, pairs, across, 0)
+    lax.fori_loop(4 * PAD // KERNEL, pairs, across, 0)
+    wide = widen(upper, early)
     written = []
-    for n, (source, target) in enumerate(((gconv_ref, gconv_hbm), (ggate_ref, ggate_hbm))):
-        written.append(pltpu.make_async_copy(source, target, writes.at[n]))
+
+    def write(source, target):
+        written.append(pltpu.make_async_copy(source, target, writes.at[len(written)]))
         written[-1].start()
+
+    write(gconv_ref, gconv_hbm)
+    write(ggate_ref, ggate_hbm)
 
     spill_copy = post.send(edge_ref, spill_ref, former)
     per_head = dot(sums_ref[...], spread_ref[...], 1, 1, EXACT)[:, 0:heads]
@@ -489,32 +553,29 @@
     turn_back[...] = jnp.zeros_like(turn_back)
     turn_back[:, 0:heads] = grad_step
     gstep_ref[...] = turn_back[...].T[0:heads, :]
+    write(gstep_ref, gstep_hbm)
     small = KERNEL * pairs
     red_out[small : small + 1, 0:heads] = jnp.sum(grad_step, axis=0, keepdims=True)
     red_out[small + 1 : small + 2, 0:heads] = jnp.sum(dlog * log_decay, axis=0, keepdims=True)
     red_out[small + 2 : small + 3, 0:heads] = per_head[0:1]
-    reds = [post.send(red_out, red_a.at[place], shard(group, peer, groups)) for peer in peers]
-    red_a[place] = red_out[...]
+    reds = exchange(under)
     coef_out[...] = jnp.concatenate([db_ref[...], dc_ref[...]], axis=1).astype(BF16)
     coefs = [post.send(coef_out, coef_all.at[head], peer) for peer in head_peers]
     coef_all[head] = coef_out[...]
+    wide += widen(under, reds)
     whole_sum(dv_out, dv_back, dv_all, dv_own, PLACES, 1.0)
     give_back(dv_own, dv_in)
-    for copy in reds:
-        copy.wait()
-    red_mid[...] = red_a[0] + red_a[1] + red_a[2] + red_a[3]
-    wide = [
-        post.send(red_mid, red_b.at[group], shard(group + away, place, groups)) for away in range(1, groups)
-    ]
-    red_b[group] = red_mid[...]
     spill_copy.wait()
     gfix_ref[...] = end_ref[...] + spill_ref[...]
+    write(gfix_ref, gfix_hbm)
     for copy in coefs:
         copy.wait()
     halves = [coef_all[2 * n].astype(F32) + coef_all[2 * n + 1].astype(F32) for n in range(2)]
     half = coef_out.shape[1] // 2
     gin_ref[...] = jnp.concatenate([halves[0][:, :half], halves[1][:, :half]], axis=1)
     gout_ref[...] = jnp.concatenate([halves[0][:, half:], halves[1][:, half:]], axis=1)
+    write(gin_ref, gin_hbm)
+    write(gout_ref, gout_hbm)
     for copy in wide:
         copy.wait()
     total = red_b[0]
@@ -525,31 +586,42 @@
         copy.wait()
 
 
-def finish_kernel(
-    dq_in, dk_in, dv_in, gconv_in, ggate_in, gfix_ref, gstep_in, gin_in, gout_in, total_ref,
-    dq_ref, dk_ref, dv_ref, gconv_ref, ggate_ref, gstep_ref, gin_ref, gout_ref, conv_ref, bias_ref, rate_ref, skip_ref,
-):
-    for source, target in ((dq_in, dq_ref), (dk_in, dk_ref), (dv_in, dv_ref)):
+def finish_kernel(ins, outs, in_bufs, out_bufs, load_sems, store_sems):
+    loads = [pltpu.make_async_copy(a, b, load_sems.at[n]) for n, (a, b) in enumerate(zip(ins, in_bufs))]
+    for load in loads:
+        load.start()
+    stores = []
+
+    def store(source, target):
+        stores.append(pltpu.make_async_copy(source, target, store_sems.at[len(stores)]))
+        stores[-1].start()
+
+    total, fix, gconv = in_bufs[0], in_bufs[1], in_bufs[2]
+    for load in loads[:3]:
+        load.wait()
+    gconv[gconv.shape[0] - PAD :, :] = fix[...].astype(BF16)
+    store(gconv, outs[3])
+    conv, *small = out_bufs[3:]
+    pairs, heads = conv.shape[1] // LANES, small[0].shape[1]
+    for lag in range(KERNEL):
+        for n in range(pairs):
+            row = KERNEL * n + lag
+            conv[lag : lag + 1, n * LANES : (n + 1) * LANES] = total[row : row + 1, :]
+    for n, ref in enumerate(small):
+        row = KERNEL * pairs + n
+        ref[...] = total[row : row + 1, 0:heads]
+    for n, ref in enumerate((conv, *small)):
+        store(ref, outs[8 + n])
+    for n in range(3, 7):
+        loads[n].wait()
+        store(in_bufs[n], outs[n + 1])
+    for n in range(3):
+        loads[7 + n].wait()
         for r in range(PLACES):
-            target[:, r * HEAD_DIM : (r + 1) * HEAD_DIM] = source[r, :, 0:HEAD_DIM]
-    for source, target in (
-        (gconv_in, gconv_ref), (ggate_in, ggate_ref), (gstep_in, gstep_ref), (gin_in, gin_ref), (gout_in, gout_ref)
-    ):
-        target[...] = source[...]
-
-    @pl.when(pl.program_id(0) == pl.num_programs(0) - 1)
-    def _():
-        rows = gconv_ref.shape[0]
-        gconv_ref[rows - PAD :, :] = gfix_ref[...].astype(BF16)
-        pairs = conv_ref.shape[1] // LANES
-        heads = bias_ref.shape[1]
-        for lag in range(KERNEL):
-            for n in range(pairs):
-                row = lag * pairs + n
-                conv_ref[lag : lag + 1, n * LANES : (n + 1) * LANES] = total_ref[row : row + 1, :]
-        for n, ref in enumerate((bias_ref, rate_ref, skip_ref)):
-            row = KERNEL * pairs + n
-            ref[...] = total_ref[row : row + 1, 0:heads]
+            unfold(in_bufs[7 + n], (r,), out_bufs[n], (), r * HEAD_DIM)
+        store(out_bufs[n], outs[n])
+    for copy in stores:
+        copy.wait()
 
 
 def local(
@@ -571,6 +643,8 @@
     full = lambda *shape: pltpu.VMEM(shape, F32)
     flat = full(PAD, channels)
     piece = lambda n: half(n, rows, head_cols)
+    slim_rows = rows * HEAD_DIM // LANES
+    slim = lambda n: half(n, slim_rows, LANES)
     red_rows = 64
     wide_shape = (rows, channels)
     small = [
@@ -580,23 +654,25 @@
     mid = pl.pallas_call(
         whole_kernel,
         in_specs=[[loose] * 8] + [loose] * 7,
-        out_specs=[loose] * 5 + [vmem] * 5,
-        out_shape=[struct((PLACES, rows, head_cols), BF16)] * 3
+        out_specs=[loose] * 9 + [vmem],
+        out_shape=[struct((PLACES, slim_rows, LANES), BF16)] * 3
         + [
             struct(wide_shape, BF16), struct(wide_shape, BF16), struct((PAD, channels), F32),
             struct((heads, rows), F32), struct((rows, LANES), F32), struct((rows, LANES), F32),
             struct((red_rows, LANES), F32),
         ],
         scratch_shapes=[
-            [pltpu.VMEM(a.shape, a.dtype) for a in small], half(*wide_shape), half(*wide_shape),
+            [pltpu.VMEM(a.shape, a.dtype) for a in small],
+            flat, full(heads, rows), full(rows, LANES), full(rows, LANES), half(*wide_shape), half(*wide_shape),
             full(PAD, rows), full(PLACES * rows // LANES, LANES), full(LANES, rows), full(rows, LANES),
             half(rows, width), half(rows, width), half(rows, width), half(rows, width),
             half(*wide_shape), half(*wide_shape), half(*wide_shape),
-            piece(PLACES), piece(PLACES), piece(PLACES), piece(PLACES),
+            slim(PLACES), slim(PLACES), slim(PLACES), slim(PLACES),
+            slim(PLACES), slim(PLACES), slim(2 * PLACES), slim(2 * PLACES), full(slim_rows, LANES),
             piece(PLACES), piece(PLACES), piece(2 * PLACES), piece(2 * PLACES),
             full(2 * PLACES, rows, head_cols), full(2 * PLACES, rows, head_cols),
-            piece(PLACES), piece(PLACES), piece(PLACES), piece(PLACES),
-            piece(PLACES), piece(PLACES), piece(PLACES),
+            slim(PLACES), slim(PLACES), slim(PLACES), slim(PLACES),
+            slim(PLACES), slim(PLACES), slim(PLACES),
             half(2 * PAD, channels), flat, full(pairs, rows, 8), full(pairs, 2, rows), full(LANES, channels),
             full(KERNEL - 1, rows, LANES), full(rows + PAD, LANES),
             full(*wide_shape), full(*wide_shape), full(*wide_shape), full(*wide_shape), full(*wide_shape),
@@ -609,7 +685,7 @@
             flat, flat, flat, flat, half(rows, LANES), half(4, rows, LANES),
             full(red_rows, LANES), full(PLACES, red_rows, LANES), full(red_rows, LANES),
             full(groups, red_rows, LANES),
-            dma(SENDS), dma(SENDS), dma(2 * PLACES), dma(2 * PLACES), dma(7), dma(3 * PLACES), dma(2), dma(8),
+            dma(SENDS), dma(SENDS), dma(2 * PLACES), dma(2 * PLACES), dma(7), dma(3 * PLACES), dma(6), dma(8),
         ],
         name="whole",
         compiler_params=pltpu.CompilerParams(
@@ -618,30 +694,24 @@
     )(
         small, keys, values, queries, attn_grad, conv_input, gate_input, mix_grad,
     )
-    steps = 4
-    tall = lambda cols: pl.BlockSpec((rows // steps, cols), lambda n: (n, 0))
-    piled = pl.BlockSpec((PLACES, rows // steps, head_cols), lambda n: (0, n, 0))
-    whole = lambda *shape: pl.BlockSpec(shape, lambda n: (0, 0))
+    dq, dk, dv, gconv, ggate, gfix, gstep, gin, gout, total = mid
+    ins = [total, gfix, gconv, ggate, gstep, gin, gout, dq, dk, dv]
+    shapes = [struct((rows, width), BF16)] * 3 + [
+        struct(wide_shape, BF16), struct(wide_shape, BF16), struct((heads, rows), F32),
+        struct((rows, LANES), F32), struct((rows, LANES), F32), struct((KERNEL, channels), F32),
+    ] + [struct((1, heads), F32)] * 3
     *outs, conv, bias, rate, skip = pl.pallas_call(
         finish_kernel,
-        grid=(steps,),
-        in_specs=[piled] * 3
-        + [
-            tall(channels), tall(channels), whole(PAD, channels), whole(heads, rows), tall(LANES), tall(LANES),
-            whole(red_rows, LANES),
+        in_specs=[[loose] * len(ins)],
+        out_specs=[[loose] * len(shapes)],
+        out_shape=[shapes],
+        scratch_shapes=[
+            [pltpu.VMEM(a.shape, a.dtype) for a in ins],
+            [pltpu.VMEM(shapes[n].shape, shapes[n].dtype) for n in (0, 1, 2, 8, 9, 10, 11)],
+            dma(len(ins)), dma(len(shapes)),
         ],
-        out_specs=[tall(width)] * 3
-        + [tall(channels), tall(channels), whole(heads, rows), tall(LANES), tall(LANES), whole(KERNEL, channels)]
-        + [whole(1, heads)] * 3,
-        out_shape=[struct((rows, width), BF16)] * 3
-        + [
-            struct(wide_shape, BF16), struct(wide_shape, BF16), struct((heads, rows), F32),
-            struct((rows, LANES), F32), struct((rows, LANES), F32), struct((KERNEL, channels), F32),
-        ]
-        + [struct((1, heads), F32)] * 3,
         name="finish",
-        compiler_params=pltpu.CompilerParams(dimension_semantics=("arbitrary",)),
-    )(*mid)
+    )(ins)[0]
     outs[5] = outs[5].T
     return (*outs, conv, bias[0], rate[0], skip[0])
 

time: 82.1 us -> 80.2 us (0.977)
  Pallas kernels: 80.5 us -> 79.2 us
    pallas_call x1, Pallas kernels: 4.88 us -> 3.65 us  [local(): pl.pallas_call(finish_kernel, in_specs=[[loose] * len(ins)], out_specs=[[...]
where the time goes in v4:
time: 80.2 us; the launch traced here: 80 us
  Pallas kernels  79.2 us (99%)
  between operations  0.84 us (1%)
    pallas_call x1, Pallas kernels, local(): pl.pallas_call(whole_kernel, in_specs=[[loose] * 8] + [loose] * 7, out_sp...  75.5 us
    pallas_call x1, Pallas kernels, local(): pl.pallas_call(finish_kernel, in_specs=[[loose] * len(ins)], out_specs=[[...  3.65 us

profile of v4, /device:TPU:0, one launch (start us, length us, event | category | flops | bytes accessed | tf_op | source)
XLA Modules:
  0.0 80.0 jit_solution(9694057900706737523)
XLA Ops:
  0.7 75.5 %whole.1 = (bf16[4,448,128]{2,1,0:T(8,128)(2,1)}, bf16[4,448,128]{2,1,0:T(8,128)(2,1)}, bf16[4,448,128]{2,1,0:T(8,128)(2,1)}, bf16[256,1792]{1,0:T(8,128)(2,1)},...) custom-call(s32[64,128]{1,0:T(8,128)} %bitcast.9, ...), custom_call_target="tpu_custom_call" | custom-call | tf_op jit(solution)/shard_map/whole/pallas_call | solution.py:654
  76.2 3.6 %finish.1 = (bf16[256,896]{1,0:T(8,128)(2,1)}, bf16[256,896]{1,0:T(8,128)(2,1)}, bf16[256,896]{1,0:T(8,128)(2,1)}, bf16[256,1792]{1,0:T(8,128)(2,1)}, bf16[256,1...) custom-call(f32[64,128]{1,0:T(8,128)} %get-tuple-element.34.ins_0_, ...), custom_call_target="tpu_custom_call" | custom-call | tf_op jit(solution)/shard_map/finish/pallas_call | solution.py:703

commit v5 on v4

--- a/solution.py
+++ b/solution.py
@@ -82,13 +82,13 @@
         mask_ref[lag - 1] = jnp.broadcast_to((since >= lag).astype(F32), mask_ref.shape[1:])
 
 
-def conv_pre(conv, tail, wt, mask_ref, xp_ref):
+def conv_pre(conv, tail, wt, mask_ref, xp_ref, lanes):
     rows = conv.shape[0]
-    xp_ref[:PAD, :] = tail.astype(F32)[PAD:]
-    xp_ref[PAD:, :] = conv.astype(F32)
-    pre = wt[0:1, :] * xp_ref[PAD:, :]
+    xp_ref[:PAD, lanes] = tail.astype(F32)[PAD:]
+    xp_ref[PAD:, lanes] = conv.astype(F32)
+    pre = wt[0:1, :] * conv.astype(F32)
     for lag in range(1, KERNEL):
-        pre = pre + wt[lag : lag + 1, :] * (xp_ref[PAD - lag : PAD - lag + rows, :] * mask_ref[lag - 1])
+        pre = pre + wt[lag : lag + 1, :] * (xp_ref[PAD - lag : PAD - lag + rows, lanes] * mask_ref[lag - 1])
     return pre
 
 
@@ -134,7 +134,7 @@
     tail_buf, wt_ref, cols_ref, rowc_ref, spread_ref, mask_ref, xp_ref,
     act_all, slope_all, dy_all, cg_all, inner_all, dx_all,
     ends_ref, a_ref, end_out, cot_out, g_out, e_in, c_in, ge_in, gc_in, chain_out, state_ref, t_out, t_all,
-    mix_bias, pair_ref, dpair_ref, dpad_ref, z_ref, u_ref, db_ref, dc_ref,
+    mix_bias, pair_ref, dpair_ref, dpad_ref, zu_ref, db_ref, dc_ref,
     sums_ref, edge_ref, end_ref, spill_ref, coef_out, coef_all, red_out, red_a, red_mid, red_b,
     sends, receives, back_sends, back_receives, loads, keeps, writes, small_loads,
 ):
@@ -253,7 +253,7 @@
     def ends(n, carry):
         lanes = pl.ds(pl.multiple_of(n * LANES, LANES), LANES)
         cols = cols_ref[n]
-        pre = conv_pre(conv_ref[:, lanes], tail_buf[:, lanes], wt_ref[:, lanes], mask_ref, xp_ref)
+        pre = conv_pre(conv_ref[:, lanes], tail_buf[:, lanes], wt_ref[:, lanes], mask_ref, xp_ref, lanes)
         sig_pre = jax.nn.sigmoid(pre)
         act = pre * sig_pre
         act_all[:, lanes] = act
@@ -309,7 +309,7 @@
 
     mix_bias[...] = jnp.where((i >= j) & ((i - j).astype(F32) <= since), 0.0, NEG_FILL)
     pair_ref[...] = dot(c_part, b_part, 1, 1)
-    for ref in (dpair_ref, z_ref, u_ref, db_ref, dc_ref, dpad_ref, red_out):
+    for ref in (dpair_ref, zu_ref, db_ref, dc_ref, dpad_ref, red_out):
         ref[...] = jnp.zeros_like(ref)
 
     def within(n, carry):
@@ -417,7 +417,7 @@
         fold(dv_all[b].astype(BF16), dv_out, (b,))
         return carry
 
-    lax.fori_loop(0, PLACES // 2, block, 0)
+    lax.fori_loop(0, 1, block, 0)
     for copy in b_copies:
         copy.wait()
     before = dot(ge_in[...].reshape(REACH * PAD, LANES), spread_ref[...], 1, 0, EXACT)
@@ -440,7 +440,7 @@
     ]
     state_ref[place] = chain_out[place]
 
-    lax.fori_loop(PLACES // 2, PLACES, block, 0)
+    lax.fori_loop(1, PLACES, block, 0)
     for b in range(PLACES):
         back_copy(dv_out, dv_back, b, PLACES + b).start()
     kept = []
@@ -460,8 +460,6 @@
         size = pair_columns(cols, 1, lower)
         enter = pair_columns(cols, 2, lower)
         to_end = pair_columns(cols, 3, lower)
-        xp_ref[:PAD, :] = tail_buf[:, lanes].astype(F32)[PAD:]
-        xp_ref[PAD:, :] = conv_ref[:, lanes].astype(F32)
         act = act_all[:, lanes]
         dy = dy_all[:, lanes]
         x_wide = (act * size).astype(BF16).astype(F32)
@@ -474,23 +472,23 @@
         ggate_ref[:, lanes] = (cg_all[:, lanes] * (inner + skip * act)).astype(BF16)
         zed = dy.astype(BF16).astype(F32) * inner - x_wide * dx
         you = dx * act
+        zu = zu_ref[...]
         for k in range(2):
             side = lower if k == 0 else ~lower
-            here = lane == 2 * n + k
             z_one = jnp.sum(jnp.where(side, zed, 0.0), axis=1, keepdims=True)
             u_one = jnp.sum(jnp.where(side, you, 0.0), axis=1, keepdims=True)
-            z_ref[...] = jnp.where(here, z_one, z_ref[...])
-            u_ref[...] = jnp.where(here, u_one, u_ref[...])
+            zu = jnp.where(lane == 2 * n + k, z_one, jnp.where(lane == LANES // 2 + 2 * n + k, u_one, zu))
+        zu_ref[...] = zu
         dc_ref[...] += dot((enter * dy).astype(BF16), state, 1, 1)
         db_ref[...] += dot((to_end * x_wide).astype(BF16), end_cot, 1, 1)
         dpre = (dx * size + skip * dy) * slope_all[:, lanes]
-        red_out[pl.ds(KERNEL * n, 1), :] = jnp.sum(dpre * xp_ref[PAD:, :], axis=0, keepdims=True)
+        red_out[pl.ds(KERNEL * n, 1), :] = jnp.sum(dpre * xp_ref[PAD:, lanes], axis=0, keepdims=True)
         dpad_ref[0, PAD : PAD + rows, :] = dpre
         grown = wt[0:1, :] * dpad_ref[0, 0 : rows + PAD, :]
         for lag in range(1, KERNEL):
             masked = dpre * mask_ref[lag - 1]
             red_out[pl.ds(KERNEL * n + lag, 1), :] = jnp.sum(
-                masked * xp_ref[PAD - lag : PAD - lag + rows, :], axis=0, keepdims=True
+                masked * xp_ref[PAD - lag : PAD - lag + rows, lanes], axis=0, keepdims=True
             )
             dpad_ref[lag, PAD : PAD + rows, :] = masked
             grown = grown + wt[lag : lag + 1, :] * dpad_ref[lag, lag : lag + rows + PAD, :]
@@ -509,7 +507,7 @@
             back_copy(source, target, b, offset + b).wait()
             out[b] = ((own_fold[...] + target[b].astype(F32)) * factor).astype(BF16)
 
-    lane = lax.broadcasted_iota(jnp.int32, (rows, heads), 1)
+    lane = lax.broadcasted_iota(jnp.int32, (rows, LANES), 1)
     for copy in state_copies:
         copy.wait()
     def exchange(part):
@@ -547,9 +545,9 @@
     spill_copy = post.send(edge_ref, spill_ref, former)
     per_head = dot(sums_ref[...], spread_ref[...], 1, 1, EXACT)[:, 0:heads]
     last_row = per_head[2:3] + through * per_head[1:2]
-    dcum = z_ref[...] + jnp.where(t == rows - 1, last_row, 0.0)
+    dcum = zu_ref[:, 0:heads] + jnp.where(t == rows - 1, last_row, 0.0)
     dlog = dot(tri, dcum, 0, 0, EXACT)
-    grad_step = (u_ref[...] - dlog * rate) * jax.nn.sigmoid(raw)
+    grad_step = (zu_ref[:, LANES // 2 : LANES // 2 + heads] - dlog * rate) * jax.nn.sigmoid(raw)
     turn_back[...] = jnp.zeros_like(turn_back)
     turn_back[:, 0:heads] = grad_step
     gstep_ref[...] = turn_back[...].T[0:heads, :]
@@ -674,14 +672,14 @@
             slim(PLACES), slim(PLACES), slim(PLACES), slim(PLACES),
             slim(PLACES), slim(PLACES), slim(PLACES),
             half(2 * PAD, channels), flat, full(pairs, rows, 8), full(pairs, 2, rows), full(LANES, channels),
-            full(KERNEL - 1, rows, LANES), full(rows + PAD, LANES),
+            full(KERNEL - 1, rows, LANES), full(rows + PAD, channels),
             full(*wide_shape), full(*wide_shape), full(*wide_shape), full(*wide_shape), full(*wide_shape),
             full(*wide_shape),
             half(PLACES, *quarter), half(PLACES, *quarter), half(*part), half(*part), full(PAD, LANES),
             half(REACH, *part), half(REACH, *part), full(REACH, PAD, LANES), full(REACH, PAD, LANES),
             half(PLACES, *quarter), half(PLACES, *quarter), full(PAD, LANES), full(PLACES, PAD, LANES),
             full(rows, rows), full(rows, rows), full(rows, rows), full(KERNEL, rows + 2 * PAD, LANES),
-            full(rows, heads), full(rows, heads), full(rows, LANES // 2), full(rows, LANES // 2),
+            full(rows, LANES), full(rows, LANES // 2), full(rows, LANES // 2),
             flat, flat, flat, flat, half(rows, LANES), half(4, rows, LANES),
             full(red_rows, LANES), full(PLACES, red_rows, LANES), full(red_rows, LANES),
             full(groups, red_rows, LANES),

time: 80.2 us -> 79.4 us (0.990)
  no operation moved by 1% of the time
where the time goes in v5:
time: 79.4 us; the launch traced here: 79.3 us
  Pallas kernels  78.5 us (99%)
  between operations  0.84 us (1%)
    pallas_call x1, Pallas kernels, local(): pl.pallas_call(whole_kernel, in_specs=[[loose] * 8] + [loose] * 7, out_sp...  74.8 us
    pallas_call x1, Pallas kernels, local(): pl.pallas_call(finish_kernel, in_specs=[[loose] * len(ins)], out_specs=[[...  3.65 us

profile of v5, /device:TPU:0, one launch (start us, length us, event | category | flops | bytes accessed | tf_op | source)
XLA Modules:
  0.0 79.3 jit_solution(5848118830204410068)
XLA Ops:
  0.7 74.8 %whole.1 = (bf16[4,448,128]{2,1,0:T(8,128)(2,1)}, bf16[4,448,128]{2,1,0:T(8,128)(2,1)}, bf16[4,448,128]{2,1,0:T(8,128)(2,1)}, bf16[256,1792]{1,0:T(8,128)(2,1)},...) custom-call(s32[64,128]{1,0:T(8,128)} %bitcast.9, ...), custom_call_target="tpu_custom_call" | custom-call | tf_op jit(solution)/shard_map/whole/pallas_call | solution.py:652
  75.5 3.6 %finish.1 = (bf16[256,896]{1,0:T(8,128)(2,1)}, bf16[256,896]{1,0:T(8,128)(2,1)}, bf16[256,896]{1,0:T(8,128)(2,1)}, bf16[256,1792]{1,0:T(8,128)(2,1)}, bf16[256,1...) custom-call(f32[64,128]{1,0:T(8,128)} %get-tuple-element.34.ins_0_, ...), custom_call_target="tpu_custom_call" | custom-call | tf_op jit(solution)/shard_map/finish/pallas_call | solution.py:701

commit v6 on v5

--- a/solution.py
+++ b/solution.py
@@ -532,6 +532,9 @@
     whole_sum(dk_out, dk_back, dk_all, dk_own, 0, SCALE)
     give_back(dk_own, dk_in)
     lax.fori_loop(4 * PAD // KERNEL, pairs, across, 0)
+    coef_out[...] = jnp.concatenate([db_ref[...], dc_ref[...]], axis=1).astype(BF16)
+    coefs = [post.send(coef_out, coef_all.at[head], peer) for peer in head_peers]
+    coef_all[head] = coef_out[...]
     wide = widen(upper, early)
     written = []
 
@@ -557,9 +560,6 @@
     red_out[small + 1 : small + 2, 0:heads] = jnp.sum(dlog * log_decay, axis=0, keepdims=True)
     red_out[small + 2 : small + 3, 0:heads] = per_head[0:1]
     reds = exchange(under)
-    coef_out[...] = jnp.concatenate([db_ref[...], dc_ref[...]], axis=1).astype(BF16)
-    coefs = [post.send(coef_out, coef_all.at[head], peer) for peer in head_peers]
-    coef_all[head] = coef_out[...]
     wide += widen(under, reds)
     whole_sum(dv_out, dv_back, dv_all, dv_own, PLACES, 1.0)
     give_back(dv_own, dv_in)

time: 79.4 us -> 79.4 us (level)
  no operation moved by 1% of the time
where the time goes in v6:
time: 79.4 us; the launch traced here: 79.3 us
  Pallas kernels  78.4 us (99%)
  between operations  0.84 us (1%)
    pallas_call x1, Pallas kernels, local(): pl.pallas_call(whole_kernel, in_specs=[[loose] * 8] + [loose] * 7, out_sp...  74.8 us
    pallas_call x1, Pallas kernels, local(): pl.pallas_call(finish_kernel, in_specs=[[loose] * len(ins)], out_specs=[[...  3.65 us

profile of v6, /device:TPU:0, one launch (start us, length us, event | category | flops | bytes accessed | tf_op | source)
XLA Modules:
  0.0 79.3 jit_solution(17945911170328505817)
XLA Ops:
  0.7 74.8 %whole.1 = (bf16[4,448,128]{2,1,0:T(8,128)(2,1)}, bf16[4,448,128]{2,1,0:T(8,128)(2,1)}, bf16[4,448,128]{2,1,0:T(8,128)(2,1)}, bf16[256,1792]{1,0:T(8,128)(2,1)},...) custom-call(s32[64,128]{1,0:T(8,128)} %bitcast.9, ...), custom_call_target="tpu_custom_call" | custom-call | tf_op jit(solution)/shard_map/whole/pallas_call | solution.py:652
  75.4 3.6 %finish.1 = (bf16[256,896]{1,0:T(8,128)(2,1)}, bf16[256,896]{1,0:T(8,128)(2,1)}, bf16[256,896]{1,0:T(8,128)(2,1)}, bf16[256,1792]{1,0:T(8,128)(2,1)}, bf16[256,1...) custom-call(f32[64,128]{1,0:T(8,128)} %get-tuple-element.34.ins_0_, ...), custom_call_target="tpu_custom_call" | custom-call | tf_op jit(solution)/shard_map/finish/pallas_call | solution.py:701
